TPU v7x, 32 devices: a 4x4x1 block of a 4x4x8 slice. The times are simulated.
32 devices in a mesh: rep: 1 (over z), tp: 4 (over y), sp: 8 (over x, core).
Axes of the slice: x: 4, y: 4, z: 1, core: 2. Of those that a mesh axis runs over, the one named last changes fastest.
The devices are a block of a 4x4x8 slice.
Arguments:
- x_in: bfloat16 [8192, 4096], P(('rep', 'sp'))
- positions: int32 [8192], P(('rep', 'sp'))
- segments: int32 [8192], P(('rep', 'sp'))
- gain_attn: float32 [4096], replicated
- w_q: bfloat16 [4096, 4096], P(None, 'tp')
- w_k: bfloat16 [4096, 1024], P(None, 'tp')
- w_v: bfloat16 [4096, 1024], P(None, 'tp')
- w_o: bfloat16 [4096, 4096], P('tp')
- gain_mlp: float32 [4096], replicated
- w_gate: bfloat16 [4096, 14336], P(None, 'tp')
- w_up: bfloat16 [4096, 14336], P(None, 'tp')
- w_down: bfloat16 [14336, 4096], P('tp')
Outputs:
- output 1: bfloat16 [8192, 4096], P(('rep', 'sp'))
- output 2: bfloat16 [8192, 32, 128], P('rep', ('tp', 'sp'))
- output 3: bfloat16 [8192, 32, 128], P('rep', ('tp', 'sp'))
All inputs are finite; a program needn't handle non-finite values.
Results may differ from a plain program's by a relative error of at most 0.00724617.
Values are sent between devices in bfloat16 or wider.
A program may use at most 768 MiB of HBM per device.

v0:
```python
import jax
import jax.numpy as jnp
from jax import lax
from jax.sharding import PartitionSpec as P

HEAD_DIM = 128
ROPE_BASE = 500000.0
NORM_EPS = 1e-5
QUERY_ROWS = 512


def rms_norm(x_f32, gain_vec):
    mean_sq = jnp.mean(x_f32 * x_f32, axis=-1, keepdims=True)
    return (x_f32 * lax.rsqrt(mean_sq + NORM_EPS) * gain_vec).astype(jnp.bfloat16)


def rope_tables(positions):
    half_dim = HEAD_DIM // 2
    inv_freq = jnp.power(jnp.float32(ROPE_BASE), -jnp.arange(half_dim, dtype=jnp.float32) * (2.0 / HEAD_DIM))
    angles = positions.astype(jnp.float32)[..., None] * inv_freq
    return jnp.cos(angles)[..., None, :], jnp.sin(angles)[..., None, :]


def rotate(t_f32, cos_t, sin_t):
    half_dim = HEAD_DIM // 2
    t_lo = t_f32[..., :half_dim]
    t_hi = t_f32[..., half_dim:]
    return jnp.concatenate([t_lo * cos_t - t_hi * sin_t, t_hi * cos_t + t_lo * sin_t], axis=-1)


def project_qkv(x_f32, positions, gain_attn, w_q, w_k, w_v):
    row_count = x_f32.shape[0]
    u_norm = rms_norm(x_f32, gain_attn)
    cos_t, sin_t = rope_tables(positions)
    q_rot = rotate(jnp.dot(u_norm, w_q, preferred_element_type=jnp.float32).reshape(row_count, -1, HEAD_DIM), cos_t, sin_t).astype(jnp.bfloat16)
    k_rot = rotate(jnp.dot(u_norm, w_k, preferred_element_type=jnp.float32).reshape(row_count, -1, HEAD_DIM), cos_t, sin_t).astype(jnp.bfloat16)
    v_proj = jnp.dot(u_norm, w_v, preferred_element_type=jnp.float32).astype(jnp.bfloat16).reshape(row_count, -1, HEAD_DIM)
    return q_rot, k_rot, v_proj


def masked_attention(q_blk, key_rows, val_rows, q_index, k_index, q_seg, k_seg):
    scores = jnp.einsum("qhgc,shc->hgqs", q_blk, key_rows, preferred_element_type=jnp.float32) * (HEAD_DIM ** -0.5)
    allowed = (q_index[:, None] >= k_index[None, :]) & (q_seg[:, None] == k_seg[None, :])
    scores = jnp.where(allowed, scores, -1e30)
    row_max = jnp.max(scores, axis=-1, keepdims=True)
    weights = jnp.exp(scores - row_max)
    prob_bf16 = (weights / jnp.sum(weights, axis=-1, keepdims=True)).astype(jnp.bfloat16)
    return jnp.einsum("hgqs,shc->qhgc", prob_bf16, val_rows, preferred_element_type=jnp.float32).astype(jnp.bfloat16)


def mlp_tail(x_mid, gain_mlp, w_gate, w_up, w_down):
    u_mlp = rms_norm(x_mid, gain_mlp)
    gate_act = jnp.dot(u_mlp, w_gate, preferred_element_type=jnp.float32)
    up_act = jnp.dot(u_mlp, w_up, preferred_element_type=jnp.float32)
    hidden = (jax.nn.silu(gate_act) * up_act).astype(jnp.bfloat16)
    return (x_mid + lax.psum(jnp.dot(hidden, w_down, preferred_element_type=jnp.float32), "tp")).astype(jnp.bfloat16)


def solution(mesh):
    sp_size = mesh.shape["sp"]
    row_spec = P(("rep", "sp"), None)
    tok_spec = P(("rep", "sp"))
    full_spec = P(None)
    col_spec = P(None, "tp")
    wrow_spec = P("tp", None)
    cache_spec = P("rep", ("tp", "sp"), None)

    def local_layer(x_in, positions, segments, gain_attn, w_q, w_k, w_v, w_o, gain_mlp, w_gate, w_up, w_down):
        rows_local = x_in.shape[0]
        tokens = rows_local * sp_size
        heads_local = w_q.shape[1] // HEAD_DIM
        kv_local = w_k.shape[1] // HEAD_DIM
        kv_repeat = max(1, sp_size // kv_local)
        heads_dev = heads_local // sp_size
        slots_dev = kv_local * kv_repeat // sp_size
        group_size = heads_dev // slots_dev
        x_f32 = x_in.astype(jnp.float32)
        q_rot, k_rot, v_proj = project_qkv(x_f32, positions, gain_attn, w_q, w_k, w_v)
        k_send = jnp.repeat(k_rot, kv_repeat, axis=1).reshape(rows_local, sp_size, slots_dev, HEAD_DIM)
        v_send = jnp.repeat(v_proj, kv_repeat, axis=1).reshape(rows_local, sp_size, slots_dev, HEAD_DIM)
        send_buf = jnp.concatenate([q_rot.reshape(rows_local, sp_size, heads_dev, HEAD_DIM), k_send, v_send], axis=2)
        recv_buf = lax.all_to_all(send_buf, "sp", 1, 0, tiled=True).reshape(tokens, heads_dev + 2 * slots_dev, HEAD_DIM)
        seg_all = lax.all_gather(segments, "sp", tiled=True)
        q_all = recv_buf[:, :heads_dev].reshape(tokens, slots_dev, group_size, HEAD_DIM)
        k_all = recv_buf[:, heads_dev:heads_dev + slots_dev]
        v_all = recv_buf[:, heads_dev + slots_dev:]
        tok_index = jnp.arange(tokens)
        block_rows = min(tokens, QUERY_ROWS)
        pieces = []
        for block_idx in range(tokens // block_rows):
            row_start = block_idx * block_rows
            row_stop = row_start + block_rows
            pieces.append(masked_attention(q_all[row_start:row_stop], k_all[:row_stop], v_all[:row_stop],
                                           tok_index[row_start:row_stop], tok_index[:row_stop],
                                           seg_all[row_start:row_stop], seg_all[:row_stop]))
        attn_heads = jnp.concatenate(pieces, axis=0).reshape(sp_size, rows_local, heads_dev, HEAD_DIM)
        attn_local = lax.all_to_all(attn_heads, "sp", 0, 2, tiled=True).reshape(rows_local, heads_local * HEAD_DIM)
        x_mid = x_f32 + lax.psum(jnp.dot(attn_local, w_o, preferred_element_type=jnp.float32), "tp")
        y_out = mlp_tail(x_mid, gain_mlp, w_gate, w_up, w_down)
        return y_out, k_all, v_all

    return jax.shard_map(local_layer, mesh=mesh,
                         in_specs=(row_spec, tok_spec, tok_spec, full_spec, col_spec, col_spec, col_spec, wrow_spec,
                                   full_spec, col_spec, col_spec, wrow_spec),
                         out_specs=(row_spec, cache_spec, cache_spec), check_vma=False)
```

profile of v0, /device:TPU:97, one launch (start us, length us, event | category | flops | bytes accessed | tf_op | source)
XLA Modules:
  0.0 1096.6 jit_solution(16068984738919527724)
XLA Ops:
  19.5 14.2 %fusion.201 = f32[1024,1024]{0,1:T(8,128)S(1)} fusion(bf16[4096,1024]{1,0:T(8,128)(2,1)} %param.16, bf16[1024,4096]{1,0:T(8,128)(2,1)} %param.12, f32[4096]{0:T(1024)S(1)} %copy-done.23, f32[1024]{0:T(1024)S(1)} %add_rsqrt_fusion.1), kind=kOutput, calls=%fused_computation.256 | convolution fusion | flops 8606711808 | bytes 20992000 | tf_op jit(solution)/shard_map/dot_general | solution.py:35
  46.0 81.8 %all_gather.3 = s32[8192]{0:T(1024)S(1)} all-gather(s32[1024]{0:T(1024)S(1)} %copy-done.13), channel_id=1, replica_groups=mesh['rep'=1,'tp'=4,'sp'=8] {'sp'}, dimensions={0}, use_global_device_ids=true | all-gather | bytes 36864 | tf_op jit(solution)/shard_map/all_gather | solution.py:83
  132.8 9.0 copy.21
  196.2 7.3 fusion.216
  216.5 7.8 fusion.217
  231.0 7.0 fusion.139
  238.0 7.4 fusion.218
  245.4 7.1 fusion.6
  252.6 7.4 fusion.133
  260.0 9.8 fusion.219
  269.8 7.6 fusion.5
  277.4 7.9 fusion.127
  285.3 8.9 fusion.220
  294.2 8.2 fusion.4
  302.4 8.3 fusion.119
  314.9 34.1 %all_to_all.30 = bf16[8,1024,1,128]{1,3,2,0:T(8,128)(2,1)S(1)} all-to-all(bf16[8,1024,1,128]{1,3,2,0:T(8,128)(2,1)S(1)} %copy.22), channel_id=1, replica_groups=mesh['rep'=1,'tp'=4,'sp'=8] {'sp'}, dimensions={0} | all-to-all | bytes 4194304 | tf_op jit(solution)/shard_map/all_to_all | solution.py:97
  349.0 14.5 %fusion.221 = f32[1024,4096]{1,0:T(8,128)} fusion(bf16[1024,1024]{0,1:T(8,128)(2,1)S(1)} %bitcast.636, bf16[1024,4096]{1,0:T(8,128)(2,1)} %param.19), kind=kOutput, calls=%fused_computation.275 | convolution fusion | flops 8589934592 | bytes 27262976 | tf_op jit(solution)/shard_map/dot_general | solution.py:98
  363.7 290.9 %all-reduce.3.cloned.1.call-done = f32[1024,4096]{1,0:T(8,128)} async-done(((f32[1024,4096]{1,0:T(8,128)}), f32[1024,4096]{1,0:T(8,128)}) %all-reduce.3.cloned.1.call-update) | async-done | bytes 16777232 | tf_op jit(solution)/shard_map/psum | solution.py:98
  654.5 9.5 multiply_reduce_fusion
  673.7 35.2 %fusion.222 = f32[1024,3584]{1,0:T(8,128)} fusion(bf16[1024,4096]{1,0:T(8,128)(2,1)S(1)} %multiply_convert_fusion, bf16[4096,3584]{1,0:T(8,128)(2,1)} %param.21), kind=kOutput, calls=%fused_computation.276 | convolution fusion | flops 30064771072 | bytes 52428800 | tf_op jit(solution)/shard_map/dot_general | solution.py:53
  708.9 36.2 %multiply_convert_fusion.1.clone.4 = bf16[1024,3584]{1,0:T(8,128)(2,1)S(1)} fusion(f32[1024,3584]{1,0:T(8,128)} %fusion.222, bf16[1024,4096]{1,0:T(8,128)(2,1)S(1)} %multiply_convert_fusion, bf16[4096,3584]{1,0:T(8,128)(2,1)} %param.22), kind=kOutput, calls=%fused_computation.19.clone.clone.clone.1 | convolution fusion | flops 30086791168 | bytes 59768832 | tf_op jit(solution)/shard_map/dot_general | solution.py:54
  745.1 36.2 %fusion.11 = f32[1024,4096]{1,0:T(8,128)} fusion(bf16[3584,4096]{1,0:T(8,128)(2,1)} %param.23, bf16[1024,3584]{1,0:T(8,128)(2,1)S(1)} %multiply_convert_fusion.1.clone.4), kind=kOutput, calls=%fused_computation.43 | convolution fusion | flops 30064771072 | bytes 53477376 | tf_op jit(solution)/shard_map/dot_general | solution.py:56
  781.3 290.2 %all-reduce.5.cloned.1.call-done = f32[1024,4096]{1,0:T(8,128)} async-done(((f32[1024,4096]{1,0:T(8,128)}), f32[1024,4096]{1,0:T(8,128)}) %all-reduce.5.cloned.1.call-update) | async-done | bytes 16777232 | tf_op jit(solution)/shard_map/psum | solution.py:56
  1071.5 17.8 %add_convert_fusion = bf16[1024,4096]{1,0:T(8,128)(2,1)} fusion(f32[1024,4096]{1,0:T(8,128)} %all-reduce.5.cloned.1.call-done, f32[1024,4096]{1,0:T(8,128)} %all-reduce.3.cloned.1.call-done, bf16[1024,4096]{1,0:T(8,128)(2,1)} %param.12), kind=kLoop, calls=%fused_computation.7 | loop fusion | flops 16777216 | bytes 50331648 | tf_op jit(solution)/shard_map/convert_element_type | solution.py:56
  (165 shorter events, 117.4 us)
Async XLA Ops:
  39.2 6.8 copy-start.13
  39.2 93.5 %all-to-all-start = ((bf16[1024,8,3,128]{0,3,2,1:T(8,128)(2,1)}), bf16[1024,8,3,128]{0,3,2,1:T(8,128)(2,1)}, u32[]{:S(2)}, u32[]{:S(2)}) async-start(bf16[1024,8,3,128]{0,3,2,1:T(8,128)(2,1)} %pad_maximum_fusion), calls=%async_computation | async-start | bytes 12582912 | tf_op jit(solution)/shard_map/all_to_all | solution.py:82
  46.0 608.5 %all-reduce.3.cloned.1.call-start = ((), (), s32[]{:S(2)}) async-start(), calls=%async_computation.2 | async-start | bytes 33554432 | tf_op jit(solution)/shard_map/psum | solution.py:98
  127.8 13.9 %copy-start.5 = (s32[8192]{0:T(1024)}, s32[8192]{0:T(1024)S(1)}, u32[]{:S(2)}) copy-start(s32[8192]{0:T(1024)S(1)} %all_gather.3) | copy-start | bytes 98308
  209.8 6.7 slice-start.11
  209.8 6.7 copy-start.11
  209.8 6.6 copy-start.17
  209.8 6.6 copy-start.21
  231.0 7.0 slice-start.12
  231.0 7.0 copy-start.10
  231.0 7.0 copy-start.16
  231.0 7.0 copy-start.20
  252.6 7.4 copy-start.6
  252.6 7.4 copy-start.9
  252.6 7.4 copy-start.15
  252.6 7.4 copy-start.19
  277.4 7.9 copy-start.8
  277.4 7.9 copy-start.14
  277.4 7.9 copy-start.18
  294.2 8.2 copy-start.7
  363.6 300.5 %copy-start.12 = (f32[4096]{0:T(1024)S(1)}, f32[4096]{0:T(1024)}, u32[]{:S(2)}) copy-start(f32[4096]{0:T(1024)} %param.20) | copy-start | bytes 49156
  363.6 707.9 %all-reduce.5.cloned.1.call-start = ((), (), s32[]{:S(2)}) async-start(), calls=%async_computation.3 | async-start | bytes 33554432 | tf_op jit(solution)/shard_map/psum | solution.py:56
  654.5 13.0 %copy-start.2 = (f32[1024,4096]{1,0:T(8,128)S(1)}, f32[1024,4096]{1,0:T(8,128)}, u32[]{:S(2)}) copy-start(f32[1024,4096]{1,0:T(8,128)} %all-reduce.3.cloned.1.call-done) | copy-start | bytes 50331652
  1071.5 17.8 %copy-start.1 = (bf16[4096,256]{1,0:T(8,128)(2,1)S(1)}, bf16[4096,256]{1,0:T(8,128)(2,1)}, u32[]{:S(2)}) copy-start(bf16[4096,256]{1,0:T(8,128)(2,1)} %param.18) | copy-start | bytes 6291460
  (16 other events, 55.0 us)
Sparse Core Ops, SparseCore 0:
  363.7 290.8 all-reduce.2
  781.4 290.0 all-reduce.4
where the time goes:
time: 1100 us
  waiting for transfers between devices  581 us (53%)
  matrix products  259 us (24%)
  blocking collectives  116 us (11%)
  other arithmetic  95.6 us (9%)
  local copies, waits for them, and re-layouts  23 us (2%)
  between operations  15 us (1%)
    psum x1, waiting for transfers between devices, local_layer(): lax.psum(jnp.dot(attn_local, w_o, preferred_element_type=jnp.float32), 'tp')  291 us
    psum x1, waiting for transfers between devices, mlp_tail(): lax.psum(jnp.dot(hidden, w_down, preferred_element_type=jnp.float32), 'tp')  290 us
    all_gather x1, blocking collectives, local_layer(): seg_all = lax.all_gather(segments, 'sp', tiled=True)  81.8 us
    dot_general x16, matrix products, masked_attention(): jnp.einsum('hgqs,shc->qhgc', prob_bf16, val_rows, preferred_element_type=...  59 us
    dot_general x16, matrix products, masked_attention(): jnp.einsum('qhgc,shc->hgqs', q_blk, key_rows, preferred_element_type=jnp....  58 us
    reduce_sum x16, other arithmetic, masked_attention(): jnp.sum(weights, axis=-1, keepdims=True)  46.6 us
    dot_general x1, matrix products, mlp_tail(): up_act = jnp.dot(u_mlp, w_up, preferred_element_type=jnp.float32)  36.2 us
    dot_general x1, matrix products, mlp_tail(): jnp.dot(hidden, w_down, preferred_element_type=jnp.float32)  36.2 us
  transfers between devices with their start and end apart: 3, of which 2 were waited for; matrix products, arithmetic and copies ran while one was open for 0% of the time, Pallas kernels for 0%

commit v1 on v0

v1 whole, which is shorter than its diff:
```python
import functools
import math

import jax
import jax.numpy as jnp
from jax import lax
from jax.experimental import pallas as pl
from jax.experimental.pallas import tpu as pltpu
from jax.sharding import PartitionSpec as P

HEAD_DIM = 128
ROPE_BASE = 500000.0
NORM_EPS = 1e-5
NUM_REQS = 2
CHUNKS = 4
KV_BLOCK = 512
FF_TILE = 512
OUT_TILE = 256
SCORE_SCALE = HEAD_DIM ** -0.5 * math.log2(math.e)
MASKED = -1e30
F32 = jnp.float32
BF16 = jnp.bfloat16


def rms_norm(x_f32, gain_vec):
    mean_sq = jnp.mean(x_f32 * x_f32, axis=-1, keepdims=True)
    return (x_f32 * lax.rsqrt(mean_sq + NORM_EPS) * gain_vec).astype(BF16)


def rope_tables(positions):
    half_dim = HEAD_DIM // 2
    inv_freq = jnp.power(F32(ROPE_BASE), -jnp.arange(half_dim, dtype=F32) * (2.0 / HEAD_DIM))
    angles = positions.astype(F32)[..., None] * inv_freq
    return jnp.cos(angles)[..., None, :], jnp.sin(angles)[..., None, :]


def rotate(t_f32, cos_t, sin_t):
    half_dim = HEAD_DIM // 2
    t_lo = t_f32[..., :half_dim]
    t_hi = t_f32[..., half_dim:]
    return jnp.concatenate([t_lo * cos_t - t_hi * sin_t, t_hi * cos_t + t_lo * sin_t], axis=-1)


def attn_kernel(group, bounds_ref, q_ref, k_ref, v_ref, first_ref, after_ref, o_ref, m_scr, l_scr, acc_scr):
    rows = q_ref.shape[0]
    block = min(KV_BLOCK, k_ref.shape[0])
    lanes = block // HEAD_DIM
    row0, first_lo, first_hi = bounds_ref[0], bounds_ref[1], bounds_ref[2]
    m_scr[...] = jnp.full_like(m_scr, MASKED)
    l_scr[...] = jnp.zeros_like(l_scr)
    acc_scr[...] = jnp.zeros_like(acc_scr)

    start = lax.div(first_lo, block)
    stop = lax.div(row0 + (rows + block - 1), block)
    plain0 = jnp.minimum(lax.div(first_hi + (block - 1), block), stop)
    plain1 = jnp.maximum(lax.div(row0 + 1, block), plain0)
    n_low = plain0 - start

    def scores(head, key_rows):
        q_one = q_ref[:, head * HEAD_DIM:(head + 1) * HEAD_DIM]
        return lax.dot_general(q_one, key_rows, (((1,), (1,)), ((), ())), preferred_element_type=F32)

    def step(j, masked):
        offset = pl.multiple_of(j * block, block)
        key_rows = k_ref[pl.ds(offset, block), :]
        val_rows = v_ref[pl.ds(offset, block), :]
        if masked:
            k_index = offset + lax.broadcasted_iota(jnp.int32, (rows, block), 1)
            q_index = row0 + lax.broadcasted_iota(jnp.int32, (rows, block), 0)
            allowed = (k_index <= q_index) & (k_index >= first_ref[...])
        raw = scores(0, key_rows)
        for head in range(group):
            s = raw * SCORE_SCALE
            if head + 1 < group:
                raw = scores(head + 1, key_rows)
            if masked:
                s = jnp.where(allowed, s, MASKED)
            m_old = m_scr[head]
            m_new = jnp.maximum(m_old, jnp.max(s, axis=1, keepdims=True))
            alpha = jnp.exp2(m_old - m_new)
            p = jnp.exp2(s - jnp.concatenate([m_new] * lanes, axis=1))
            part = p[:, :HEAD_DIM]
            for i in range(1, lanes):
                part = part + p[:, i * HEAD_DIM:(i + 1) * HEAD_DIM]
            m_scr[head] = m_new
            l_scr[head] = alpha * l_scr[head] + part
            acc_scr[head] = alpha * acc_scr[head] + jnp.dot(p.astype(BF16), val_rows, preferred_element_type=F32)

    def plain_step(j, carry):
        step(j, False)
        return carry

    def masked_step(i, carry):
        step(jnp.where(i < n_low, start + i, plain1 + i - n_low), True)
        return carry

    lax.fori_loop(plain0, plain1, plain_step, 0)
    lax.fori_loop(0, n_low + stop - plain1, masked_step, 0)
    for head in range(group):
        total = jnp.sum(l_scr[head], axis=1, keepdims=True)
        o_ref[:, head * HEAD_DIM:(head + 1) * HEAD_DIM] = (acc_scr[head] / total).astype(BF16)


def attention_chunk(bounds, q_rot, kv_all, first_rows, chunk, rows, kv_local, after):
    tokens = kv_all.shape[0]
    width = q_rot.shape[1] // kv_local
    group = width // HEAD_DIM
    flops = 4 * rows * q_rot.shape[1] * tokens // 2
    return pl.pallas_call(
        functools.partial(attn_kernel, group),
        out_shape=jax.ShapeDtypeStruct((rows, q_rot.shape[1]), BF16),
        grid_spec=pltpu.PrefetchScalarGridSpec(
            num_scalar_prefetch=1,
            grid=(kv_local,),
            in_specs=[
                pl.BlockSpec((rows, width), lambda g, b: (chunk, g)),
                pl.BlockSpec((tokens, HEAD_DIM), lambda g, b: (0, g)),
                pl.BlockSpec((tokens, HEAD_DIM), lambda g, b: (0, kv_local + g)),
                pl.BlockSpec((rows, 1), lambda g, b: (chunk, 0)),
                pl.BlockSpec(memory_space=pl.ANY),
            ],
            out_specs=pl.BlockSpec((rows, width), lambda g, b: (0, g)),
            scratch_shapes=[pltpu.VMEM((group, rows, HEAD_DIM), F32)] * 3,
        ),
        compiler_params=pltpu.CompilerParams(dimension_semantics=("arbitrary",), vmem_limit_bytes=40 * 2 ** 20),
        cost_estimate=pl.CostEstimate(flops=3 * flops, bytes_accessed=2 * kv_all.size, transcendentals=flops // 256),
        name=f"attn{chunk}",
    )(bounds, q_rot, kv_all, kv_all, first_rows, after)


def out_proj_kernel(a_ref, w_ref, x_ref, after_ref, o_ref, ssq_ref):
    parts, slabs = a_ref.shape[0], w_ref.shape[0]
    total = x_ref[...].astype(F32)
    acc = None
    for j in range(parts):
        w_cols = jnp.concatenate([w_ref[s, j] for s in range(slabs)], axis=0)
        term = jnp.dot(a_ref[j], w_cols, preferred_element_type=F32)
        acc = term if acc is None else acc + term
    total = total + acc
    o_ref[...] = total
    squares = total * total
    part = squares[:, :128]
    for i in range(1, squares.shape[1] // 128):
        part = part + squares[:, i * 128:(i + 1) * 128]

    @pl.when(pl.program_id(0) == 0)
    def _():
        ssq_ref[...] = part

    @pl.when(pl.program_id(0) > 0)
    def _():
        ssq_ref[...] += part


def out_proj(attn_all, wo_cols, x_cols, chunk, after):
    parts, rows, depth = attn_all.shape
    slabs, _, slab_rows, cols = wo_cols.shape
    tile = min(OUT_TILE, cols)
    return pl.pallas_call(
        out_proj_kernel,
        out_shape=(jax.ShapeDtypeStruct((rows, cols), F32), jax.ShapeDtypeStruct((rows, 128), F32)),
        grid=(cols // tile,),
        in_specs=[
            pl.BlockSpec((parts, rows, depth), lambda n: (0, 0, 0)),
            pl.BlockSpec((slabs, parts, slab_rows, tile), lambda n: (0, 0, 0, n)),
            pl.BlockSpec((rows, tile), lambda n: (chunk, n)),
            pl.BlockSpec(memory_space=pl.ANY),
        ],
        out_specs=(pl.BlockSpec((rows, tile), lambda n: (0, n)), pl.BlockSpec((rows, 128), lambda n: (0, 0))),
        compiler_params=pltpu.CompilerParams(dimension_semantics=("arbitrary",), vmem_limit_bytes=40 * 2 ** 20),
        cost_estimate=pl.CostEstimate(flops=2 * rows * parts * depth * cols, bytes_accessed=2 * wo_cols.size, transcendentals=0),
        name=f"outproj{chunk}",
    )(attn_all, wo_cols, x_cols, after)


def mlp_kernel(u_ref, wg_ref, wu_ref, wd_ref, after_ref, o_ref):
    parts, rows, depth = u_ref.shape
    cols = o_ref.shape[2]

    def project(w_ref):
        acc = None
        for j in range(parts):
            term = jnp.dot(u_ref[j], w_ref[j * depth:(j + 1) * depth, :], preferred_element_type=F32)
            acc = term if acc is None else acc + term
        return acc

    hidden = (jax.nn.silu(project(wg_ref)) * project(wu_ref)).astype(BF16)

    @pl.when(pl.program_id(0) == 0)
    def _():
        for j in range(o_ref.shape[0]):
            o_ref[j] = jnp.dot(hidden, wd_ref[:, j * cols:(j + 1) * cols], preferred_element_type=F32)

    @pl.when(pl.program_id(0) > 0)
    def _():
        for j in range(o_ref.shape[0]):
            o_ref[j] += jnp.dot(hidden, wd_ref[:, j * cols:(j + 1) * cols], preferred_element_type=F32)


def mlp_partial(u_all, w_gate, w_up, w_down, chunk, after):
    parts, rows, depth = u_all.shape
    ff_local = w_gate.shape[1]
    tile = FF_TILE
    model = w_down.shape[1]
    return pl.pallas_call(
        mlp_kernel,
        out_shape=jax.ShapeDtypeStruct((parts, rows, model // parts), F32),
        grid=(ff_local // tile,),
        in_specs=[
            pl.BlockSpec((parts, rows, depth), lambda i: (0, 0, 0)),
            pl.BlockSpec((parts * depth, tile), lambda i: (0, i)),
            pl.BlockSpec((parts * depth, tile), lambda i: (0, i)),
            pl.BlockSpec((tile, model), lambda i: (i, 0)),
            pl.BlockSpec(memory_space=pl.ANY),
        ],
        out_specs=pl.BlockSpec((parts, rows, model // parts), lambda i: (0, 0, 0)),
        compiler_params=pltpu.CompilerParams(dimension_semantics=("arbitrary",), vmem_limit_bytes=56 * 2 ** 20),
        cost_estimate=pl.CostEstimate(flops=6 * rows * model * ff_local, bytes_accessed=6 * model * ff_local,
                                      transcendentals=rows * ff_local),
        name=f"mlp{chunk}",
    )(u_all, w_gate, w_up, w_down, after)


def pipeline_order(chunks):
    order = []
    for tick in range(chunks + 3):
        if tick < chunks:
            order.append(("attn", tick))
        if 1 <= tick <= chunks:
            order.append(("out", tick - 1))
        if 3 <= tick:
            order.append(("mlp", tick - 3))
    return order


def solution(mesh):
    sp_size = mesh.shape["sp"]
    tp_size = mesh.shape["tp"]
    row_spec = P(("rep", "sp"), None)
    tok_spec = P(("rep", "sp"))
    full_spec = P(None)
    col_spec = P(None, "tp")
    wrow_spec = P("tp", None)
    cache_spec = P("rep", ("tp", "sp"), None)

    def local_layer(x_in, positions, segments, gain_attn, w_q, w_k, w_v, w_o, gain_mlp, w_gate, w_up, w_down):
        rows_local, model = x_in.shape
        kv_local = w_k.shape[1] // HEAD_DIM
        heads_local = w_q.shape[1] // HEAD_DIM
        kv_repeat = sp_size // kv_local
        rows = rows_local // CHUNKS
        cols = model // tp_size
        sp_rank = lax.axis_index("sp")
        tp_rank = lax.axis_index("tp")
        row_base = sp_rank * rows_local

        below = jnp.sum(segments[:, None] < jnp.arange(NUM_REQS)[None, :], axis=0, dtype=jnp.int32)
        starts = lax.psum(below, "sp")
        first_rows = jnp.sum(jnp.where(segments[:, None] == jnp.arange(NUM_REQS)[None, :], starts[None, :], 0), axis=1,
                             dtype=jnp.int32)

        x_f32 = x_in.astype(F32)
        u_norm = rms_norm(x_f32, gain_attn)
        cos_t, sin_t = rope_tables(positions)
        k_rot = rotate(jnp.dot(u_norm, w_k, preferred_element_type=F32).reshape(rows_local, -1, HEAD_DIM), cos_t, sin_t).astype(BF16)
        v_proj = jnp.dot(u_norm, w_v, preferred_element_type=F32).astype(BF16)
        kv_own = jnp.concatenate([k_rot.reshape(rows_local, -1), v_proj], axis=1)
        kv_all = lax.all_gather(kv_own, "sp", tiled=True)
        q_rot = rotate(jnp.dot(u_norm, w_q, preferred_element_type=F32).reshape(rows_local, -1, HEAD_DIM), cos_t, sin_t).astype(BF16)
        q_rot = q_rot.reshape(rows_local, -1)
        slot_head = sp_rank // kv_repeat
        k_cache = lax.dynamic_slice_in_dim(kv_all, slot_head * HEAD_DIM, HEAD_DIM, axis=1)[:, None, :]
        v_cache = lax.dynamic_slice_in_dim(kv_all, (kv_local + slot_head) * HEAD_DIM, HEAD_DIM, axis=1)[:, None, :]

        slab_rows = heads_local * HEAD_DIM // sp_size
        slab = lax.dynamic_slice_in_dim(w_o, sp_rank * slab_rows, slab_rows, axis=0)
        slab = jnp.transpose(slab.reshape(slab_rows, tp_size, cols), (1, 0, 2))
        slab = lax.all_to_all(slab, "tp", 0, 0, tiled=True)
        wo_cols = lax.all_gather(slab, "sp")
        x_cols = lax.dynamic_slice_in_dim(x_in, tp_rank * cols, cols, axis=1)
        gain_cols = lax.dynamic_slice_in_dim(gain_mlp, tp_rank * cols, cols, axis=0)

        attn_all, x_mid, u_all, y_parts = {}, {}, {}, {}
        after = q_rot
        for stage, chunk in pipeline_order(CHUNKS):
            row0 = chunk * rows
            if stage == "attn":
                bounds = jnp.stack([row_base + row0, first_rows[row0], first_rows[row0 + rows - 1]])
                after = attention_chunk(bounds, q_rot, kv_all, first_rows[:, None], chunk, rows, kv_local, after)
                attn_all[chunk] = lax.all_gather(after, "tp")
            elif stage == "out":
                x_mid[chunk], ssq = out_proj(attn_all[chunk], wo_cols, x_cols, chunk, after)
                sum_sq = lax.psum(jnp.sum(ssq, axis=1), "tp")
                u_own = (x_mid[chunk] * lax.rsqrt(sum_sq[:, None] / model + NORM_EPS) * gain_cols).astype(BF16)
                u_all[chunk] = lax.all_gather(u_own, "tp")
                after = u_own
            else:
                after = mlp_partial(u_all[chunk], w_gate, w_up, w_down, chunk, after)
                down = lax.psum_scatter(after, "tp", scatter_dimension=0, tiled=False)
                y_parts[chunk] = lax.all_gather((x_mid[chunk] + down).astype(BF16), "tp")
        pieces = [jnp.transpose(y_parts[chunk], (1, 0, 2)).reshape(rows, model) for chunk in range(CHUNKS)]
        y_out = jnp.concatenate(pieces, axis=0)
        return y_out, k_cache, v_cache

    return jax.shard_map(local_layer, mesh=mesh,
                         in_specs=(row_spec, tok_spec, tok_spec, full_spec, col_spec, col_spec, col_spec, wrow_spec,
                                   full_spec, col_spec, col_spec, wrow_spec),
                         out_specs=(row_spec, cache_spec, cache_spec), check_vma=False)
```

time: 1100 us -> 735 us (0.67); the launches traced: 1100 us -> 720 us
  waiting for transfers between devices: 581 us -> 304 us
  matrix products: 259 us -> 20.5 us
  Pallas kernels: 0 us -> 197 us
  local copies, waits for them, and re-layouts: 23 us -> 79.2 us
  blocking collectives: 116 us -> 60.6 us
  other arithmetic: 95.6 us -> 41.9 us
    psum x2 -> x0, waiting for transfers between devices: 581 us -> none  [the longest x1 291 us: local_layer(): lax.psum(jnp.dot(attn_local, w_o, preferred_element_type=jnp.float32), 'tp')]
    dot_general x39 -> x3, matrix products: 259 us -> 20.5 us  [the longest x1 14.3 us: local_layer(): jnp.dot(u_norm, w_q, preferred_element_type=F32)]
    pallas_call x0 -> x12, Pallas kernels: none -> 197 us  [the longest x4 148 us: mlp_partial(): pl.pallas_call(mlp_kernel, out_shape=jax.ShapeDtypeStruct((parts, rows, m...]
    all_gather x0 -> x14, waiting for transfers between devices: none -> 176 us  [the longest x4 102 us: local_layer(): y_parts[chunk] = lax.all_gather((x_mid[chunk] + down).astype(BF16), 'tp')]
    reduce_scatter x0 -> x4, waiting for transfers between devices: none -> 125 us  [local_layer(): down = lax.psum_scatter(after, 'tp', scatter_dimension=0, tiled=False)]
    all_gather x1 -> x0, blocking collectives: 81.8 us -> none  [local_layer(): seg_all = lax.all_gather(segments, 'sp', tiled=True)]
    unnamed x49 -> x85, local copies, waits for them, and re-layouts: 7 us -> 55.1 us
    reduce_sum x16 -> x6, other arithmetic: 46.6 us -> 0.65 us  [the longest x4 0.44 us: local_layer(): sum_sq = lax.psum(jnp.sum(ssq, axis=1), 'tp')]
  transfers between devices with their start and end apart: 3 -> 18, of which waited for: 2 -> 12; matrix products, arithmetic and copies ran while one was open for 0% -> 10% of each run, Pallas kernels for 0% -> 27%
where the time goes in v1:
time: 735 us; the launch traced here: 720 us
  waiting for transfers between devices  304 us (41%)
  Pallas kernels  197 us (27%)
  local copies, waits for them, and re-layouts  79.2 us (11%)
  blocking collectives  60.6 us (8%)
  other arithmetic  41.9 us (6%)
  matrix products  20.5 us (3%)
  between operations  15 us (2%)
    pallas_call x4, Pallas kernels, mlp_partial(): pl.pallas_call(mlp_kernel, out_shape=jax.ShapeDtypeStruct((parts, rows, m...  148 us
    reduce_scatter x4, waiting for transfers between devices, local_layer(): down = lax.psum_scatter(after, 'tp', scatter_dimension=0, tiled=False)  125 us
    all_gather x4, waiting for transfers between devices, local_layer(): y_parts[chunk] = lax.all_gather((x_mid[chunk] + down).astype(BF16), 'tp')  102 us
    unnamed x85, local copies, waits for them, and re-layouts  55.1 us
    all_gather x4, waiting for transfers between devices, local_layer(): attn_all[chunk] = lax.all_gather(after, 'tp')  52 us
    pallas_call x4, Pallas kernels, attention_chunk(): pl.pallas_call(functools.partial(attn_kernel, group), out_shape=jax.Shape...  30.9 us
    psum x4, blocking collectives, local_layer(): sum_sq = lax.psum(jnp.sum(ssq, axis=1), 'tp')  30.1 us
    all_to_all x1, blocking collectives, local_layer(): slab = lax.all_to_all(slab, 'tp', 0, 0, tiled=True)  20.6 us
  transfers between devices with their start and end apart: 18, of which 12 were waited for; matrix products, arithmetic and copies ran while one was open for 10% of the time, Pallas kernels for 27%

profile of v1, /device:TPU:97, one launch (start us, length us, event | category | flops | bytes accessed | tf_op | source)
XLA Modules:
  0.0 720.1 jit_solution(16317514888401299202)
XLA Ops:
  28.8 20.6 %all_to_all.5 = bf16[4,128,1024]{1,2,0:T(8,128)(2,1)S(1)} all-to-all(bf16[4,128,1024]{1,2,0:T(8,128)(2,1)S(1)} %bitcast.89), channel_id=1, replica_groups=mesh['rep'=1,'tp'=4,'sp'=8] {'tp'}, dimensions={0} | all-to-all | bytes 2097152 | tf_op jit(solution)/shard_map/all_to_all | solution.py:278
  51.0 9.9 %psum.35 = s32[2]{0:T(128)S(1)} all-reduce(s32[2]{0:T(128)S(1)} %fusion.8), channel_id=1, replica_groups=mesh['rep'=1,'tp'=4,'sp'=8] {'sp'}, use_global_device_ids=true, to_apply=%region_1.0 | all-reduce | flops 2 | bytes 16 | tf_op jit(solution)/shard_map/psum | solution.py:258
  60.9 14.3 %fusion.12 = f32[1024,1024]{0,1:T(8,128)S(1)} fusion(bf16[4096,1024]{1,0:T(8,128)(2,1)} %param.16, bf16[1024,4096]{1,0:T(8,128)(2,1)} %param.12, f32[4096]{0:T(1024)S(1)} %copy-done.38, f32[1024]{0:T(1024)S(1)} %add_rsqrt_fusion), kind=kOutput, calls=%fused_computation.49 | convolution fusion | flops 8606711808 | bytes 20992000 | tf_op jit(solution)/shard_map/dot_general | solution.py:269
  95.4 10.4 %attn0.1.after_ref = bf16[256,1024]{1,0:T(8,128)(2,1)} custom-call(s32[3]{0:T(128)S(1)} %pad_add_fusion.bounds_ref, bf16[1024,1024]{1,0:T(8,128)(2,1)S(1)} %bitcast.77, bf16[8192,512]{1,0:T(8,128)(2,1)S(1)} %copy-done.19, bf16[8192,512]{1,0:T(8,128)(2,1)S(1)} %copy-done.19, s32[1024,1]{1,0:T(8,128)S(1)} %copy.59.first_ref, bf16[1024,1024]{1,0:T(8,128)(2,1)S(1)} %bitcast.78), custom_call_target="tpu_custom_call" | custom-call | flops 12884901888 | bytes 8388608 | tf_op jit(solution)/shard_map/attn0/pallas_call | solution.py:109
  127.2 29.8 %all-gather.30.cloned.1.call-done = bf16[1024,1024]{1,0:T(8,128)(2,1)} async-done(((bf16[256,1024]{1,0:T(8,128)(2,1)}), bf16[1024,1024]{1,0:T(8,128)(2,1)}) %all-gather.30.cloned.1.call-update) | async-done | bytes 2097168 | tf_op jit(solution)/shard_map/all_gather | solution.py:290
  166.3 7.6 %psum.36 = f32[256]{0:T(256)S(1)} all-reduce(f32[256]{0:T(256)S(1)} %reduce_sum.66), channel_id=1, replica_groups=mesh['rep'=1,'tp'=4,'sp'=8] {'tp'}, use_global_device_ids=true, to_apply=%region_5.6 | all-reduce | flops 256 | bytes 2048 | tf_op jit(solution)/shard_map/psum | solution.py:293
  181.9 7.4 %attn2.1.after_ref = bf16[256,1024]{1,0:T(8,128)(2,1)S(1)} custom-call(s32[3]{0:T(128)S(1)} %pad_add_fusion.2.bounds_ref, bf16[1024,1024]{1,0:T(8,128)(2,1)S(1)} %bitcast.80, bf16[8192,512]{1,0:T(8,128)(2,1)S(1)} %copy-done.21, bf16[8192,512]{1,0:T(8,128)(2,1)S(1)} %copy-done.21, s32[1024,1]{1,0:T(8,128)S(1)} %copy-done.30, bf16[256,1024]{1,0:T(8,128)(2,1)S(1)} %copy-done.26), custom_call_target="tpu_custom_call" | custom-call | flops 12884901888 | bytes 8388608 | tf_op jit(solution)/shard_map/attn2/pallas_call | solution.py:109
  202.5 7.4 %psum.37 = f32[256]{0:T(256)S(1)} all-reduce(f32[256]{0:T(256)S(1)} %reduce_sum.67), channel_id=1, replica_groups=mesh['rep'=1,'tp'=4,'sp'=8] {'tp'}, use_global_device_ids=true, to_apply=%region_7.8 | all-reduce | flops 256 | bytes 2048 | tf_op jit(solution)/shard_map/psum | solution.py:293
  218.0 7.4 %attn3.1.after_ref = bf16[256,1024]{1,0:T(8,128)(2,1)S(1)} custom-call(s32[3]{0:T(128)S(1)} %pad_add_fusion.3.bounds_ref, bf16[1024,1024]{1,0:T(8,128)(2,1)S(1)} %bitcast.81, bf16[8192,512]{1,0:T(8,128)(2,1)S(1)} %copy-done.22, bf16[8192,512]{1,0:T(8,128)(2,1)S(1)} %copy-done.22, s32[1024,1]{1,0:T(8,128)S(1)} %copy-done.31, bf16[256,1024]{1,0:T(8,128)(2,1)S(1)} %copy-done.27), custom_call_target="tpu_custom_call" | custom-call | flops 12884901888 | bytes 8388608 | tf_op jit(solution)/shard_map/attn3/pallas_call | solution.py:109
  227.1 22.2 %all-gather.36.cloned.1.call-done = bf16[1024,1024]{1,0:T(8,128)(2,1)} async-done(((bf16[256,1024]{1,0:T(8,128)(2,1)}), bf16[1024,1024]{1,0:T(8,128)(2,1)}) %all-gather.36.cloned.1.call-update) | async-done | bytes 2097168 | tf_op jit(solution)/shard_map/all_gather | solution.py:290
  259.6 7.6 %psum.38 = f32[256]{0:T(256)S(1)} all-reduce(f32[256]{0:T(256)S(1)} %reduce_sum.68), channel_id=1, replica_groups=mesh['rep'=1,'tp'=4,'sp'=8] {'tp'}, use_global_device_ids=true, to_apply=%region_9.10 | all-reduce | flops 256 | bytes 2048 | tf_op jit(solution)/shard_map/psum | solution.py:293
  268.3 10.7 %all-gather.34.cloned.1.call-done = bf16[1024,1024]{1,0:T(8,128)(2,1)} async-done(((bf16[256,1024]{1,0:T(8,128)(2,1)}), bf16[1024,1024]{1,0:T(8,128)(2,1)}) %all-gather.34.cloned.1.call-update) | async-done | bytes 2097168 | tf_op jit(solution)/shard_map/all_gather | solution.py:295
  279.0 37.0 %mlp0.1.after_ref = f32[4,256,1024]{2,1,0:T(8,128)} custom-call(bf16[4,256,1024]{2,1,0:T(8,128)(2,1)} %bitcast.90, bf16[4096,3584]{1,0:T(8,128)(2,1)} %wg_ref.7, bf16[4096,3584]{1,0:T(8,128)(2,1)} %wu_ref.7, bf16[3584,4096]{1,0:T(8,128)(2,1)} %wd_ref.7, bf16[256,1024]{1,0:T(8,128)(2,1)} %multiply_convert_fusion.1.after_ref), custom_call_target="tpu_custom_call" | custom-call | flops 22548578304 | bytes 88080384 | tf_op jit(solution)/shard_map/mlp0/pallas_call | solution.py:205
  326.5 7.6 %psum.39 = f32[256]{0:T(256)S(1)} all-reduce(f32[256]{0:T(256)S(1)} %reduce_sum.69), channel_id=1, replica_groups=mesh['rep'=1,'tp'=4,'sp'=8] {'tp'}, use_global_device_ids=true, to_apply=%region_12.13 | all-reduce | flops 256 | bytes 2048 | tf_op jit(solution)/shard_map/psum | solution.py:293
  341.4 36.9 %mlp1.1.after_ref = f32[4,256,1024]{2,1,0:T(8,128)} custom-call(bf16[4,256,1024]{2,1,0:T(8,128)(2,1)} %bitcast.91, bf16[4096,3584]{1,0:T(8,128)(2,1)} %wg_ref.7, bf16[4096,3584]{1,0:T(8,128)(2,1)} %wu_ref.7, bf16[3584,4096]{1,0:T(8,128)(2,1)} %wd_ref.7, bf16[256,1024]{1,0:T(8,128)(2,1)} %multiply_convert_fusion.after_ref), custom_call_target="tpu_custom_call" | custom-call | flops 22548578304 | bytes 88080384 | tf_op jit(solution)/shard_map/mlp1/pallas_call | solution.py:205
  379.1 37.1 %mlp2.1.after_ref = f32[4,256,1024]{2,1,0:T(8,128)} custom-call(bf16[4,256,1024]{2,1,0:T(8,128)(2,1)} %bitcast.92, bf16[4096,3584]{1,0:T(8,128)(2,1)} %wg_ref.7, bf16[4096,3584]{1,0:T(8,128)(2,1)} %wu_ref.7, bf16[3584,4096]{1,0:T(8,128)(2,1)} %wd_ref.7, f32[4,256,1024]{2,1,0:T(8,128)} %mlp1.1.after_ref), custom_call_target="tpu_custom_call" | custom-call | flops 22548578304 | bytes 88080384 | tf_op jit(solution)/shard_map/mlp2/pallas_call | solution.py:205
  416.2 37.0 %mlp3.1 = f32[4,256,1024]{2,1,0:T(8,128)} custom-call(bf16[4,256,1024]{2,1,0:T(8,128)(2,1)} %bitcast.93, bf16[4096,3584]{1,0:T(8,128)(2,1)} %wg_ref.7, bf16[4096,3584]{1,0:T(8,128)(2,1)} %wu_ref.7, bf16[3584,4096]{1,0:T(8,128)(2,1)} %wd_ref.7, f32[4,256,1024]{2,1,0:T(8,128)} %mlp2.1.after_ref), custom_call_target="tpu_custom_call" | custom-call | flops 22548578304 | bytes 88080384 | tf_op jit(solution)/shard_map/mlp3/pallas_call | solution.py:205
  456.7 37.1 %reduce-scatter.5.cloned.1.call-done = f32[1,256,1024]{2,1,0:T(8,128)} async-done(((f32[4,256,1024]{2,1,0:T(8,128)}), f32[1,256,1024]{2,1,0:T(8,128)}) %reduce-scatter.5.cloned.1.call-update) | async-done | bytes 1048592 | tf_op jit(solution)/shard_map/reduce_scatter | solution.py:299
  496.1 44.1 %reduce-scatter.11.cloned.1.call-done = f32[1,256,1024]{2,1,0:T(8,128)} async-done(((f32[4,256,1024]{2,1,0:T(8,128)}), f32[1,256,1024]{2,1,0:T(8,128)}) %reduce-scatter.11.cloned.1.call-update) | async-done | bytes 1048592 | tf_op jit(solution)/shard_map/reduce_scatter | solution.py:299
  542.5 44.0 %reduce-scatter.9.cloned.1.call-done = f32[1,256,1024]{2,1,0:T(8,128)} async-done(((f32[4,256,1024]{2,1,0:T(8,128)}), f32[1,256,1024]{2,1,0:T(8,128)}) %reduce-scatter.9.cloned.1.call-update) | async-done | bytes 1048592 | tf_op jit(solution)/shard_map/reduce_scatter | solution.py:299
  593.2 22.4 %all-gather.46.cloned.1.call-done = bf16[1024,1024]{1,0:T(8,128)(2,1)} async-done(((bf16[256,1024]{1,0:T(8,128)(2,1)}), bf16[1024,1024]{1,0:T(8,128)(2,1)}) %all-gather.46.cloned.1.call-update) | async-done | bytes 2097168 | tf_op jit(solution)/shard_map/all_gather | solution.py:300
  618.9 26.2 %all-gather.40.cloned.1.call-done = bf16[1024,1024]{1,0:T(8,128)(2,1)} async-done(((bf16[256,1024]{1,0:T(8,128)(2,1)}), bf16[1024,1024]{1,0:T(8,128)(2,1)}) %all-gather.40.cloned.1.call-update) | async-done | bytes 2097168 | tf_op jit(solution)/shard_map/all_gather | solution.py:300
  648.2 26.9 %all-gather.54.cloned.1.call-done = bf16[1024,1024]{1,0:T(8,128)(2,1)} async-done(((bf16[256,1024]{1,0:T(8,128)(2,1)}), bf16[1024,1024]{1,0:T(8,128)(2,1)}) %all-gather.54.cloned.1.call-update) | async-done | bytes 2097168 | tf_op jit(solution)/shard_map/all_gather | solution.py:300
  678.2 26.3 %all-gather.50.cloned.1.call-done = bf16[1024,1024]{1,0:T(8,128)(2,1)} async-done(((bf16[256,1024]{1,0:T(8,128)(2,1)}), bf16[1024,1024]{1,0:T(8,128)(2,1)}) %all-gather.50.cloned.1.call-update) | async-done | bytes 2097168 | tf_op jit(solution)/shard_map/all_gather | solution.py:300
  (182 shorter events, 167.4 us)
Async XLA Ops:
  7.2 84.9 %all-gather.28.cloned.1.call-start = ((), (), s32[]{:S(2)}) async-start(), calls=%async_computation.5 | async-start | bytes 9437184 | tf_op jit(solution)/shard_map/all_gather | solution.py:268
  26.7 100.4 %all-gather.32.cloned.1.call-start = ((), (), s32[]{:S(2)}) async-start(), calls=%async_computation.11 | async-start | bytes 9437184 | tf_op jit(solution)/shard_map/all_gather | solution.py:279
  28.1 22.8 %copy-start.35 = (s32[1024]{0:T(1024)S(1)}, s32[1024]{0:T(1024)}, u32[]{:S(2)}) copy-start(s32[1024]{0:T(1024)} %param.14) | copy-start | bytes 12292
  50.8 106.2 %all-gather.30.cloned.1.call-start = ((), (), s32[]{:S(2)}) async-start(), calls=%async_computation.10 | async-start | bytes 2621440 | tf_op jit(solution)/shard_map/all_gather | solution.py:290
  89.5 18.1 %copy-start.23 = (bf16[128,8,8,128]{3,1,2,0:T(8,128)(2,1)}, bf16[128,8,8,128]{3,1,2,0:T(8,128)(2,1)S(1)}, u32[]{:S(2)}) copy-start(bf16[128,8,8,128]{3,1,2,0:T(8,128)(2,1)S(1)} %copy.83) | copy-start | bytes 6291460
  105.9 86.3 %all-gather.38.cloned.1.call-start = ((), (), s32[]{:S(2)}) async-start(), calls=%async_computation.14 | async-start | bytes 2621440 | tf_op jit(solution)/shard_map/all_gather | solution.py:290
  116.8 132.5 %all-gather.36.cloned.1.call-start = ((), (), s32[]{:S(2)}) async-start(), calls=%async_computation.13 | async-start | bytes 2621440 | tf_op jit(solution)/shard_map/all_gather | solution.py:290
  166.2 23.1 %copy-start.6 = (f32[256,1024]{1,0:T(8,128)}, f32[256,1024]{1,0:T(8,128)S(1)}, u32[]{:S(2)}) copy-start(f32[256,1024]{1,0:T(8,128)S(1)} %get-tuple-element.11) | copy-start | bytes 3145732
  190.1 88.9 %all-gather.34.cloned.1.call-start = ((), (), s32[]{:S(2)}) async-start(), calls=%async_computation.12 | async-start | bytes 2621440 | tf_op jit(solution)/shard_map/all_gather | solution.py:295
  190.7 125.2 %all-gather.44.cloned.1.call-start = ((), (), s32[]{:S(2)}) async-start(), calls=%async_computation.17 | async-start | bytes 2621440 | tf_op jit(solution)/shard_map/all_gather | solution.py:290
  202.4 23.0 %copy-start.8 = (f32[256,1024]{1,0:T(8,128)}, f32[256,1024]{1,0:T(8,128)S(1)}, u32[]{:S(2)}) copy-start(f32[256,1024]{1,0:T(8,128)S(1)} %get-tuple-element.13) | copy-start | bytes 3145732
  226.2 115.2 %all-gather.42.cloned.1.call-start = ((), (), s32[]{:S(2)}) async-start(), calls=%async_computation.16 | async-start | bytes 2621440 | tf_op jit(solution)/shard_map/all_gather | solution.py:295
  227.0 152.1 %all-gather.48.cloned.1.call-start = ((), (), s32[]{:S(2)}) async-start(), calls=%async_computation.19 | async-start | bytes 2621440 | tf_op jit(solution)/shard_map/all_gather | solution.py:295
  268.2 148.0 %all-gather.52.cloned.1.call-start = ((), (), s32[]{:S(2)}) async-start(), calls=%async_computation.21 | async-start | bytes 2621440 | tf_op jit(solution)/shard_map/all_gather | solution.py:295
  336.3 117.7 %reduce-scatter.7.cloned.1.call-start = ((), (), s32[]{:S(2)}) async-start(), calls=%async_computation.7 | async-start | bytes 5242880 | tf_op jit(solution)/shard_map/reduce_scatter | solution.py:299
  378.4 115.5 %reduce-scatter.5.cloned.1.call-start = ((), (), s32[]{:S(2)}) async-start(), calls=%async_computation.6 | async-start | bytes 5242880 | tf_op jit(solution)/shard_map/reduce_scatter | solution.py:299
  379.0 161.2 %reduce-scatter.11.cloned.1.call-start = ((), (), s32[]{:S(2)}) async-start(), calls=%async_computation.9 | async-start | bytes 5242880 | tf_op jit(solution)/shard_map/reduce_scatter | solution.py:299
  453.3 40.6 %copy-start.7 = (f32[256,1024]{1,0:T(8,128)S(1)}, f32[256,1024]{1,0:T(8,128)}, u32[]{:S(2)}) copy-start(f32[256,1024]{1,0:T(8,128)} %copy-done.6) | copy-start | bytes 3145732
  453.3 133.2 %reduce-scatter.9.cloned.1.call-start = ((), (), s32[]{:S(2)}) async-start(), calls=%async_computation.8 | async-start | bytes 5242880 | tf_op jit(solution)/shard_map/reduce_scatter | solution.py:299
  453.9 161.7 %all-gather.46.cloned.1.call-start = ((), (), s32[]{:S(2)}) async-start(), calls=%async_computation.18 | async-start | bytes 2621440 | tf_op jit(solution)/shard_map/all_gather | solution.py:300
  456.6 83.7 %copy-start.11 = (f32[256,1024]{1,0:T(8,128)S(1)}, f32[256,1024]{1,0:T(8,128)}, u32[]{:S(2)}) copy-start(f32[256,1024]{1,0:T(8,128)} %copy-done.10) | copy-start | bytes 3145732
  456.6 188.4 %all-gather.40.cloned.1.call-start = ((), (), s32[]{:S(2)}) async-start(), calls=%async_computation.15 | async-start | bytes 2621440 | tf_op jit(solution)/shard_map/all_gather | solution.py:300
  496.1 179.0 %all-gather.54.cloned.1.call-start = ((), (), s32[]{:S(2)}) async-start(), calls=%async_computation.22 | async-start | bytes 2621440 | tf_op jit(solution)/shard_map/all_gather | solution.py:300
  542.4 162.1 %all-gather.50.cloned.1.call-start = ((), (), s32[]{:S(2)}) async-start(), calls=%async_computation.20 | async-start | bytes 2621440 | tf_op jit(solution)/shard_map/all_gather | solution.py:300
  (33 other events, 102.8 us)
Sparse Core Ops, SparseCore 0:
  26.9 51.3 all-gather.27
  79.9 47.2 all-gather.31
  129.3 27.6 all-gather.29
  158.4 28.7 all-gather.37
  190.2 59.0 all-gather.35
  250.8 28.1 all-gather.33
  281.1 30.4 all-gather.43
  313.2 28.1 all-gather.41
  343.0 27.9 all-gather.47
  372.4 27.9 all-gather.51
  402.7 44.3 reduce-scatter.6
  449.8 44.0 reduce-scatter.4
  496.2 44.0 reduce-scatter.10
  542.4 44.0 reduce-scatter.8
  587.9 27.6 all-gather.45
  617.0 27.9 all-gather.39
  647.1 27.9 all-gather.53
  676.5 27.9 all-gather.49

commit v2 on v1

v2 whole, which is shorter than its diff:
```python
import functools
import math

import jax
import jax.numpy as jnp
from jax import lax
from jax.experimental import pallas as pl
from jax.experimental.pallas import tpu as pltpu
from jax.sharding import PartitionSpec as P


HEAD_DIM = 128
ROPE_BASE = 500000.0
NORM_EPS = 1e-5
NUM_REQS = 2
CHUNKS = 4
KV_BLOCK = 512
FF_TILE = 512
OUT_TILE = 256
VMEM_GRANT = 63_000_000
SCORE_SCALE = HEAD_DIM ** -0.5 * math.log2(math.e)
MASKED = -1e30
F32 = jnp.float32
BF16 = jnp.bfloat16


def rms_norm(x_f32, gain_vec):
    mean_sq = jnp.mean(x_f32 * x_f32, axis=-1, keepdims=True)
    return (x_f32 * lax.rsqrt(mean_sq + NORM_EPS) * gain_vec).astype(BF16)


def rope_tables(positions):
    half_dim = HEAD_DIM // 2
    inv_freq = jnp.power(F32(ROPE_BASE), -jnp.arange(half_dim, dtype=F32) * (2.0 / HEAD_DIM))
    angles = positions.astype(F32)[..., None] * inv_freq
    return jnp.cos(angles)[..., None, :], jnp.sin(angles)[..., None, :]


def rotate(t_f32, cos_t, sin_t):
    half_dim = HEAD_DIM // 2
    t_lo = t_f32[..., :half_dim]
    t_hi = t_f32[..., half_dim:]
    return jnp.concatenate([t_lo * cos_t - t_hi * sin_t, t_hi * cos_t + t_lo * sin_t], axis=-1)


def attn_kernel(group, bounds_ref, q_ref, k_ref, v_ref, first_ref, *refs):
    o_ref, q_scr, m_scr, l_scr, acc_scr = refs[-5:]
    rows = q_ref.shape[0]
    block = min(KV_BLOCK, k_ref.shape[0])
    row0, first_lo, first_hi = bounds_ref[0], bounds_ref[1], bounds_ref[2]
    m_scr[...] = jnp.full_like(m_scr, MASKED)
    l_scr[...] = jnp.zeros_like(l_scr)
    acc_scr[...] = jnp.zeros_like(acc_scr)
    for head in range(group):
        q_one = q_ref[:, head * HEAD_DIM:(head + 1) * HEAD_DIM]
        q_scr[head] = jnp.transpose(q_one.astype(F32)).astype(BF16)

    start = lax.div(first_lo, block)
    stop = lax.div(row0 + (rows + block - 1), block)
    plain0 = jnp.minimum(lax.div(first_hi + (block - 1), block), stop)
    plain1 = jnp.maximum(lax.div(row0 + 1, block), plain0)
    n_low = plain0 - start

    def step(j, masked):
        offset = pl.multiple_of(j * block, block)
        key_rows = k_ref[pl.ds(offset, block), :]
        val_cols = jnp.transpose(v_ref[pl.ds(offset, block), :])
        if masked:
            k_index = offset + lax.broadcasted_iota(jnp.int32, (block, rows), 0)
            q_index = row0 + lax.broadcasted_iota(jnp.int32, (block, rows), 1)
            allowed = (k_index <= q_index) & (k_index >= first_ref[...])
        raw = jnp.dot(key_rows, q_scr[0], preferred_element_type=F32)
        for head in range(group):
            s = raw * SCORE_SCALE
            if head + 1 < group:
                raw = jnp.dot(key_rows, q_scr[head + 1], preferred_element_type=F32)
            if masked:
                s = jnp.where(allowed, s, MASKED)
            m_old = m_scr[head]
            m_new = jnp.maximum(m_old, jnp.max(s, axis=0, keepdims=True))
            alpha = jnp.exp2(m_old - m_new)
            p = jnp.exp2(s - m_new)
            m_scr[head] = m_new
            l_scr[head] = alpha * l_scr[head] + jnp.sum(p.reshape(block // 8, 8, rows), axis=0)
            acc_scr[head] = alpha * acc_scr[head] + jnp.dot(val_cols, p.astype(BF16), preferred_element_type=F32)

    def plain_step(j, carry):
        step(j, False)
        return carry

    def masked_step(i, carry):
        step(jnp.where(i < n_low, start + i, plain1 + i - n_low), True)
        return carry

    lax.fori_loop(plain0, plain1, plain_step, 0)
    lax.fori_loop(0, n_low + stop - plain1, masked_step, 0)
    for head in range(group):
        total = jnp.sum(l_scr[head], axis=0, keepdims=True)
        o_ref[:, head * HEAD_DIM:(head + 1) * HEAD_DIM] = jnp.transpose(acc_scr[head] / total).astype(BF16)


def attention_chunk(bounds, q_rot, kv_all, first_rows, chunk, rows, kv_local, after):
    tokens = kv_all.shape[0]
    width = q_rot.shape[1] // kv_local
    group = width // HEAD_DIM
    flops = 4 * rows * q_rot.shape[1] * tokens
    return pl.pallas_call(
        functools.partial(attn_kernel, group),
        out_shape=jax.ShapeDtypeStruct((rows, q_rot.shape[1]), BF16),
        grid_spec=pltpu.PrefetchScalarGridSpec(
            num_scalar_prefetch=1,
            grid=(kv_local,),
            in_specs=[
                pl.BlockSpec((rows, width), lambda g, b: (chunk, g)),
                pl.BlockSpec((tokens, HEAD_DIM), lambda g, b: (0, g)),
                pl.BlockSpec((tokens, HEAD_DIM), lambda g, b: (0, kv_local + g)),
                pl.BlockSpec((1, rows), lambda g, b: (0, chunk)),
            ] + [pl.BlockSpec(memory_space=pl.ANY)] * len(after),
            out_specs=pl.BlockSpec((rows, width), lambda g, b: (0, g)),
            scratch_shapes=[
                pltpu.VMEM((group, HEAD_DIM, rows), BF16),
                pltpu.VMEM((group, 1, rows), F32),
                pltpu.VMEM((group, 8, rows), F32),
                pltpu.VMEM((group, HEAD_DIM, rows), F32),
            ],
        ),
        compiler_params=pltpu.CompilerParams(dimension_semantics=("arbitrary",), vmem_limit_bytes=VMEM_GRANT),
        cost_estimate=pl.CostEstimate(flops=2 * flops, bytes_accessed=2 * kv_all.size, transcendentals=flops // 512),
    )(bounds, q_rot, kv_all, kv_all, first_rows, *after)


def out_proj_kernel(parts, *refs):
    a_refs, (w_ref, x_ref), (o_ref, ssq_ref) = refs[:parts], refs[parts:parts + 2], refs[-2:]
    slabs = w_ref.shape[0]
    acc = None
    for j in range(parts):
        w_cols = jnp.concatenate([w_ref[s, j] for s in range(slabs)], axis=0)
        term = jnp.dot(a_refs[j][...], w_cols, preferred_element_type=F32)
        acc = term if acc is None else acc + term
    total = x_ref[...].astype(F32) + acc
    o_ref[...] = total
    squares = total * total
    part = squares[:, :128]
    for i in range(1, squares.shape[1] // 128):
        part = part + squares[:, i * 128:(i + 1) * 128]

    @pl.when(pl.program_id(0) == 0)
    def _():
        ssq_ref[...] = part

    @pl.when(pl.program_id(0) > 0)
    def _():
        ssq_ref[...] += part


def out_proj(attn_parts, wo_cols, x_cols, chunk, after):
    parts = len(attn_parts)
    rows, depth = attn_parts[0].shape
    slabs, _, slab_rows, cols = wo_cols.shape
    tile = min(OUT_TILE, cols)
    return pl.pallas_call(
        functools.partial(out_proj_kernel, parts),
        out_shape=(jax.ShapeDtypeStruct((rows, cols), F32), jax.ShapeDtypeStruct((rows, 128), F32)),
        grid=(cols // tile,),
        in_specs=[pl.BlockSpec((rows, depth), lambda n: (0, 0))] * parts + [
            pl.BlockSpec((slabs, parts, slab_rows, tile), lambda n: (0, 0, 0, n)),
            pl.BlockSpec((rows, tile), lambda n: (chunk, n)),
        ] + [pl.BlockSpec(memory_space=pl.ANY)] * len(after),
        out_specs=(pl.BlockSpec((rows, tile), lambda n: (0, n)), pl.BlockSpec((rows, 128), lambda n: (0, 0))),
        compiler_params=pltpu.CompilerParams(dimension_semantics=("arbitrary",), vmem_limit_bytes=VMEM_GRANT),
        cost_estimate=pl.CostEstimate(flops=2 * rows * parts * depth * cols, bytes_accessed=2 * wo_cols.size, transcendentals=0),
    )(*attn_parts, wo_cols, x_cols, *after)


def mlp_kernel(parts, rank_ref, *refs):
    u_refs, (wg_ref, wu_ref, wd_ref), o_ref = refs[:parts], refs[parts:parts + 3], refs[-1]
    depth = u_refs[0].shape[1]
    cols = o_ref.shape[2]

    def project(w_ref):
        acc = None
        for j in range(parts):
            owner = lax.rem(rank_ref[0] + j, parts)
            w_rows = w_ref[pl.ds(pl.multiple_of(owner * depth, depth), depth), :]
            term = jnp.dot(u_refs[j][...], w_rows, preferred_element_type=F32)
            acc = term if acc is None else acc + term
        return acc

    hidden = (jax.nn.silu(project(wg_ref)) * project(wu_ref)).astype(BF16)

    @pl.when(pl.program_id(0) == 0)
    def _():
        for j in range(o_ref.shape[0]):
            o_ref[j] = jnp.dot(hidden, wd_ref[:, j * cols:(j + 1) * cols], preferred_element_type=F32)

    @pl.when(pl.program_id(0) > 0)
    def _():
        for j in range(o_ref.shape[0]):
            o_ref[j] += jnp.dot(hidden, wd_ref[:, j * cols:(j + 1) * cols], preferred_element_type=F32)


def mlp_partial(rank, u_parts, w_gate, w_up, w_down, after):
    if isinstance(u_parts, list):
        parts = len(u_parts)
        rows, depth = u_parts[0].shape
        u_specs = [pl.BlockSpec((rows, depth), lambda i, r: (0, 0))] * parts
    else:
        parts, rows, depth = u_parts.shape
        u_specs = [pl.BlockSpec((None, rows, depth), lambda i, r, j=j: (j, 0, 0)) for j in range(parts)]
        u_parts = [u_parts] * parts
    ff_local = w_gate.shape[1]
    tile = FF_TILE
    model = w_down.shape[1]
    return pl.pallas_call(
        functools.partial(mlp_kernel, parts),
        out_shape=jax.ShapeDtypeStruct((parts, rows, model // parts), F32),
        grid_spec=pltpu.PrefetchScalarGridSpec(
            num_scalar_prefetch=1,
            grid=(ff_local // tile,),
            in_specs=u_specs + [
                pl.BlockSpec((parts * depth, tile), lambda i, r: (0, i)),
                pl.BlockSpec((parts * depth, tile), lambda i, r: (0, i)),
                pl.BlockSpec((tile, model), lambda i, r: (i, 0)),
            ] + [pl.BlockSpec(memory_space=pl.ANY)] * len(after),
            out_specs=pl.BlockSpec((parts, rows, model // parts), lambda i, r: (0, 0, 0)),
        ),
        compiler_params=pltpu.CompilerParams(dimension_semantics=("arbitrary",), vmem_limit_bytes=VMEM_GRANT),
        cost_estimate=pl.CostEstimate(flops=6 * rows * model * ff_local, bytes_accessed=6 * model * ff_local,
                                      transcendentals=rows * ff_local),
    )(rank, *u_parts, w_gate, w_up, w_down, *after)


def join_kernel(parts, rank_ref, *refs):
    part_refs, o_ref = refs[:parts], refs[-1]
    cols = part_refs[0].shape[1]
    for j in range(parts):
        owner = lax.rem(rank_ref[0] + j, parts)
        o_ref[:, pl.ds(pl.multiple_of(owner * cols, cols), cols)] = part_refs[j][...]


def join(rank, y_parts, y_out, chunk, chunks):
    parts = len(y_parts)
    rows, cols = y_parts[0].shape
    in_specs = [pl.BlockSpec((rows, cols), lambda i, r: (0, 0))] * parts
    operands = [rank, *y_parts]
    aliases = {}
    if y_out is not None:
        aliases = {len(operands): 0}
        in_specs = in_specs + [pl.BlockSpec(memory_space=pl.ANY)]
        operands.append(y_out)
    return pl.pallas_call(
        functools.partial(join_kernel, parts),
        out_shape=jax.ShapeDtypeStruct((rows * chunks, parts * cols), BF16),
        grid_spec=pltpu.PrefetchScalarGridSpec(
            num_scalar_prefetch=1,
            grid=(1,),
            in_specs=in_specs,
            out_specs=pl.BlockSpec((rows, parts * cols), lambda i, r: (chunk, 0)),
        ),
        input_output_aliases=aliases,
        compiler_params=pltpu.CompilerParams(dimension_semantics=("arbitrary",), vmem_limit_bytes=VMEM_GRANT),
        cost_estimate=pl.CostEstimate(flops=0, bytes_accessed=4 * rows * parts * cols, transcendentals=0),
    )(*operands)


def ring_gather(own, axis, size, forward):
    def shifted(block, shift):
        return lax.ppermute(block, axis, [(i, (i + shift) % size) for i in range(size)])

    if size != 4:
        return [own] + [shifted(own, -k) for k in range(1, size)]
    before = shifted(own, 1)
    behind = shifted(own, -1)
    opposite = shifted(before, 1) if forward else shifted(behind, -1)
    return [own, behind, opposite, before]


def pipeline_order(chunks):
    order = [("attn", 0), ("attn", 1)]
    for chunk in range(2, chunks):
        order += [("attn", chunk), ("out", chunk - 2)]
    order += [("out", chunks - 2), ("mlp", 0), ("out", chunks - 1)]
    return order + [("mlp", chunk) for chunk in range(1, chunks)]


def solution(mesh):
    sp_size = mesh.shape["sp"]
    tp_size = mesh.shape["tp"]
    row_spec = P(("rep", "sp"), None)
    tok_spec = P(("rep", "sp"))
    full_spec = P(None)
    col_spec = P(None, "tp")
    wrow_spec = P("tp", None)
    cache_spec = P("rep", ("tp", "sp"), None)

    def local_layer(x_in, positions, segments, gain_attn, w_q, w_k, w_v, w_o, gain_mlp, w_gate, w_up, w_down):
        rows_local, model = x_in.shape
        kv_local = w_k.shape[1] // HEAD_DIM
        heads_local = w_q.shape[1] // HEAD_DIM
        kv_repeat = sp_size // kv_local
        rows = rows_local // CHUNKS
        cols = model // tp_size
        sp_rank = lax.axis_index("sp")
        tp_rank = lax.axis_index("tp")
        row_base = sp_rank * rows_local

        below = jnp.sum(segments[:, None] < jnp.arange(NUM_REQS)[None, :], axis=0, dtype=jnp.int32)
        starts = lax.psum(below, "sp")
        first_rows = jnp.sum(jnp.where(segments[:, None] == jnp.arange(NUM_REQS)[None, :], starts[None, :], 0), axis=1,
                             dtype=jnp.int32)

        x_f32 = x_in.astype(F32)
        u_norm = rms_norm(x_f32, gain_attn)
        cos_t, sin_t = rope_tables(positions)
        k_rot = rotate(jnp.dot(u_norm, w_k, preferred_element_type=F32).reshape(rows_local, -1, HEAD_DIM), cos_t, sin_t).astype(BF16)
        v_proj = jnp.dot(u_norm, w_v, preferred_element_type=F32).astype(BF16)
        kv_own = jnp.concatenate([k_rot.reshape(rows_local, -1), v_proj], axis=1)
        kv_all = lax.all_gather(kv_own, "sp", tiled=True)
        q_rot = rotate(jnp.dot(u_norm, w_q, preferred_element_type=F32).reshape(rows_local, -1, HEAD_DIM), cos_t, sin_t).astype(BF16)
        q_rot = q_rot.reshape(rows_local, -1)
        slot_head = sp_rank // kv_repeat
        k_cache = lax.dynamic_slice_in_dim(kv_all, slot_head * HEAD_DIM, HEAD_DIM, axis=1)[:, None, :]
        v_cache = lax.dynamic_slice_in_dim(kv_all, (kv_local + slot_head) * HEAD_DIM, HEAD_DIM, axis=1)[:, None, :]

        slab_rows = heads_local * HEAD_DIM // sp_size
        slab = lax.dynamic_slice_in_dim(w_o, sp_rank * slab_rows, slab_rows, axis=0)
        slabs = [lax.dynamic_slice_in_dim(slab, tp_rank * cols, cols, axis=1)]
        for k in range(1, tp_size):
            block = lax.dynamic_slice_in_dim(slab, lax.rem(tp_rank + tp_size - k, tp_size) * cols, cols, axis=1)
            slabs.append(lax.ppermute(block, "tp", [(i, (i + tp_size - k) % tp_size) for i in range(tp_size)]))
        wo_cols = lax.all_gather(jnp.stack(slabs), "sp")
        x_cols = lax.dynamic_slice_in_dim(x_in, tp_rank * cols, cols, axis=1)
        gain_cols = lax.dynamic_slice_in_dim(gain_mlp, tp_rank * cols, cols, axis=0)

        rank = jnp.reshape(tp_rank, (1,)).astype(jnp.int32)
        rank_zero = jnp.zeros((1,), jnp.int32)
        attn_all, x_mid, u_all, y_own, y_all = {}, {}, {}, {}, {}
        after = [q_rot]
        for stage, chunk in pipeline_order(CHUNKS):
            row0 = chunk * rows
            forward = chunk % 2 == 0
            if stage == "attn":
                if chunk >= 2:
                    after = after + [attn_all[chunk - 2][1], attn_all[chunk - 2][-1]]
                bounds = jnp.stack([row_base + row0, first_rows[row0], first_rows[row0 + rows - 1]])
                attn_own = attention_chunk(bounds, q_rot, kv_all, first_rows[None, :], chunk, rows, kv_local, after)
                attn_all[chunk] = ring_gather(attn_own, "tp", tp_size, forward)
                after = [attn_own]
            elif stage == "out":
                if chunk == CHUNKS - 1 and CHUNKS >= 4 and tp_size == 4:
                    after = after + [u_all[2][1], u_all[2][-1]]
                x_mid[chunk], ssq = out_proj(attn_all[chunk], wo_cols, x_cols, chunk, after)
                sum_sq = lax.psum(jnp.sum(ssq, axis=1), "tp")
                u_own = (x_mid[chunk] * lax.rsqrt(sum_sq[:, None] / model + NORM_EPS) * gain_cols).astype(BF16)
                on_queue = chunk < 2
                u_all[chunk] = lax.all_gather(u_own, "tp") if on_queue else ring_gather(u_own, "tp", tp_size, forward)
                after = [u_own]
            else:
                if chunk >= 2:
                    after = after + [u_all[chunk][1], u_all[chunk][-1], y_own[chunk - 2]]
                if chunk + 1 < CHUNKS and isinstance(u_all[chunk + 1], list):
                    after = after + [u_all[chunk + 1][1], u_all[chunk + 1][-1]]
                if chunk >= 3:
                    after = after + [y_all[chunk - 3][1], y_all[chunk - 3][-1]]
                own_rank = rank if isinstance(u_all[chunk], list) else rank_zero
                if chunk == 0:
                    after = after + [attn_all[CHUNKS - 1][1], attn_all[CHUNKS - 1][-1]]
                partial = mlp_partial(own_rank, u_all[chunk], w_gate, w_up, w_down, after)
                down = lax.psum_scatter(partial, "tp", scatter_dimension=0, tiled=False)
                y_own[chunk] = (x_mid[chunk] + down).astype(BF16)
                y_all[chunk] = ring_gather(y_own[chunk], "tp", tp_size, forward)
                after = [partial]
        y_out = None
        for chunk in range(CHUNKS):
            y_out = join(rank, y_all[chunk], y_out, chunk, CHUNKS)
        return y_out, k_cache, v_cache

    return jax.shard_map(local_layer, mesh=mesh,
                         in_specs=(row_spec, tok_spec, tok_spec, full_spec, col_spec, col_spec, col_spec, wrow_spec,
                                   full_spec, col_spec, col_spec, wrow_spec),
                         out_specs=(row_spec, cache_spec, cache_spec), check_vma=False)
```

time: 735 us -> 741 us (level)
  the two profiles are of different devices: /device:TPU:97 before, /device:TPU:102 now
where the time goes in v2:
time: 741 us; the launch traced here: 732 us
  Pallas kernels  334 us (45%)
  waiting for transfers between devices  195 us (26%)
  blocking collectives  48.7 us (7%)
  other arithmetic  45.6 us (6%)
  local copies, waits for them, and re-layouts  37.5 us (5%)
  starting transfers between devices  35 us (5%)
  matrix products  20.3 us (3%)
  between operations  14.9 us (2%)
    pallas_call x4, Pallas kernels, mlp_partial(): pl.pallas_call(functools.partial(mlp_kernel, parts), out_shape=jax.ShapeD...  150 us
    pallas_call x4, Pallas kernels, attention_chunk(): pl.pallas_call(functools.partial(attn_kernel, group), out_shape=jax.Shape...  143 us
    reduce_scatter x4, waiting for transfers between devices, local_layer(): down = lax.psum_scatter(partial, 'tp', scatter_dimension=0, tiled=False)  131 us
    ppermute x30, waiting for transfers between devices, shifted(): lax.ppermute(block, axis, [(i, (i + shift) % size) for i in range(size)])  53.6 us
    psum x4, blocking collectives, local_layer(): sum_sq = lax.psum(jnp.sum(ssq, axis=1), 'tp')  41.2 us
    pallas_call x4, Pallas kernels, out_proj(): pl.pallas_call(functools.partial(out_proj_kernel, parts), out_shape=(jax....  28.5 us
    ppermute x30, starting transfers between devices, shifted(): lax.ppermute(block, axis, [(i, (i + shift) % size) for i in range(size)])  27.3 us
    unnamed x98, local copies, waits for them, and re-layouts  24.7 us
  transfers between devices with their start and end apart: 41, of which 14 were waited for; matrix products, arithmetic and copies ran while one was open for 9% of the time, Pallas kernels for 44%

profile of v2, /device:TPU:102, one launch (start us, length us, event | category | flops | bytes accessed | tf_op | source)
XLA Modules:
  0.0 731.7 jit_solution(17325917123754941544)
XLA Ops:
  48.3 7.5 %psum.35 = s32[2]{0:T(128)S(1)} all-reduce(s32[2]{0:T(128)S(1)} %fusion.8), channel_id=1, replica_groups=mesh['rep'=1,'tp'=4,'sp'=8] {'sp'}, use_global_device_ids=true, to_apply=%region_1.0 | all-reduce | flops 2 | bytes 16 | tf_op jit(solution)/shard_map/psum | solution.py:308
  55.7 14.2 %fusion.12 = f32[1024,1024]{0,1:T(8,128)S(1)} fusion(bf16[4096,1024]{1,0:T(8,128)(2,1)} %param.16, bf16[1024,4096]{1,0:T(8,128)(2,1)} %param.12, f32[4096]{0:T(1024)S(1)} %copy-done.45, f32[1024]{0:T(1024)S(1)} %add_rsqrt_fusion), kind=kOutput, calls=%fused_computation.49 | convolution fusion | flops 8606711808 | bytes 20992000 | tf_op jit(solution)/shard_map/dot_general | solution.py:319
  96.0 34.8 %shard_map.139.refs_0_ = bf16[256,1024]{1,0:T(8,128)(2,1)} custom-call(s32[3]{0:T(128)} %pad_add_fusion.1.bounds_ref, bf16[1024,1024]{1,0:T(8,128)(2,1)} %bitcast.62, bf16[8192,512]{1,0:T(8,128)(2,1)} %all-gather.8.cloned.1.call-done.k_ref.v_ref, bf16[8192,512]{1,0:T(8,128)(2,1)} %all-gather.8.cloned.1.call-done.k_ref.v_ref, s32[1,1024]{1,0:T(1,128)} %bitcast.72, ...), custom_call_target="tpu_custom_call" | custom-call | flops 17179869184 | bytes 8388608 | tf_op jit(solution)/shard_map/pallas_call | solution.py:107
  133.3 34.7 %shard_map.140.refs_0_ = bf16[256,1024]{1,0:T(8,128)(2,1)} custom-call(s32[3]{0:T(128)} %pad_add_fusion.3.bounds_ref, bf16[1024,1024]{1,0:T(8,128)(2,1)} %bitcast.64, bf16[8192,512]{1,0:T(8,128)(2,1)} %all-gather.8.cloned.1.call-done.k_ref.v_ref, bf16[8192,512]{1,0:T(8,128)(2,1)} %all-gather.8.cloned.1.call-done.k_ref.v_ref, s32[1,1024]{1,0:T(1,128)} %bitcast.73, ...), custom_call_target="tpu_custom_call" | custom-call | flops 17179869184 | bytes 8388608 | tf_op jit(solution)/shard_map/pallas_call | solution.py:107
  169.9 36.9 %shard_map.141.refs_6_.refs_0_ = bf16[256,1024]{1,0:T(8,128)(2,1)} custom-call(s32[3]{0:T(128)} %pad_add_fusion.2.bounds_ref, bf16[1024,1024]{1,0:T(8,128)(2,1)} %bitcast.65, bf16[8192,512]{1,0:T(8,128)(2,1)} %all-gather.8.cloned.1.call-done.k_ref.v_ref, bf16[8192,512]{1,0:T(8,128)(2,1)} %all-gather.8.cloned.1.call-done.k_ref.v_ref, s32[1,1024]{1,0:T(1,128)} %bitcast.74, ...), custom_call_target="tpu_custom_call" | custom-call | flops 17179869184 | bytes 8388608 | tf_op jit(solution)/shard_map/pallas_call | solution.py:107
  207.6 7.2 shard_map.142
  215.8 10.7 %psum.36 = f32[256]{0:T(256)S(1)} all-reduce(f32[256]{0:T(256)S(1)} %reduce_sum.66), channel_id=1, replica_groups=mesh['rep'=1,'tp'=4,'sp'=8] {'tp'}, use_global_device_ids=true, to_apply=%region_5.6 | all-reduce | flops 256 | bytes 2048 | tf_op jit(solution)/shard_map/psum | solution.py:353
  240.3 37.0 %shard_map.143.refs_6_.refs_0_ = bf16[256,1024]{1,0:T(8,128)(2,1)} custom-call(s32[3]{0:T(128)} %pad_add_fusion.bounds_ref, bf16[1024,1024]{1,0:T(8,128)(2,1)} %bitcast.66, bf16[8192,512]{1,0:T(8,128)(2,1)} %all-gather.8.cloned.1.call-done.k_ref.v_ref, bf16[8192,512]{1,0:T(8,128)(2,1)} %all-gather.8.cloned.1.call-done.k_ref.v_ref, s32[1,1024]{1,0:T(1,128)} %bitcast.75, ...), custom_call_target="tpu_custom_call" | custom-call | flops 17179869184 | bytes 8388608 | tf_op jit(solution)/shard_map/pallas_call | solution.py:107
  277.3 7.1 shard_map.144
  286.2 11.2 %psum.37 = f32[256]{0:T(256)S(1)} all-reduce(f32[256]{0:T(256)S(1)} %reduce_sum.67), channel_id=1, replica_groups=mesh['rep'=1,'tp'=4,'sp'=8] {'tp'}, use_global_device_ids=true, to_apply=%region_7.8 | all-reduce | flops 256 | bytes 2048 | tf_op jit(solution)/shard_map/psum | solution.py:353
  303.1 7.1 shard_map.145
  311.2 10.1 %psum.38 = f32[256]{0:T(256)S(1)} all-reduce(f32[256]{0:T(256)S(1)} %reduce_sum.68), channel_id=1, replica_groups=mesh['rep'=1,'tp'=4,'sp'=8] {'tp'}, use_global_device_ids=true, to_apply=%region_9.10 | all-reduce | flops 256 | bytes 2048 | tf_op jit(solution)/shard_map/psum | solution.py:353
  324.4 37.6 %shard_map.146.refs_6_ = f32[4,256,1024]{2,1,0:T(8,128)} custom-call(s32[1]{0:T(128)} %constant.111.clone.1.rank_ref, bf16[4,256,1024]{2,1,0:T(8,128)(2,1)} %bitcast.51, bf16[4,256,1024]{2,1,0:T(8,128)(2,1)} %bitcast.52, bf16[4,256,1024]{2,1,0:T(8,128)(2,1)} %bitcast.53, bf16[4,256,1024]{2,1,0:T(8,128)(2,1)} %bitcast.54, bf16[4096,3584]{1,0:T(8,128)(2,1)} %refs_4_.7, ...), custom_call_target="tpu_custom_call" | custom-call | flops 22548578304 | bytes 88080384 | tf_op jit(solution)/shard_map/pallas_call | solution.py:214
  365.3 7.0 collective-permute-done.9.refs_2_
  379.5 7.1 shard_map.147
  387.6 9.2 %psum.39 = f32[256]{0:T(256)S(1)} all-reduce(f32[256]{0:T(256)S(1)} %reduce_sum.69), channel_id=1, replica_groups=mesh['rep'=1,'tp'=4,'sp'=8] {'tp'}, use_global_device_ids=true, to_apply=%region_11.12 | all-reduce | flops 256 | bytes 2048 | tf_op jit(solution)/shard_map/psum | solution.py:353
  399.0 37.5 %shard_map.148.refs_7_ = f32[4,256,1024]{2,1,0:T(8,128)} custom-call(s32[1]{0:T(128)} %constant.111.clone.1.rank_ref, bf16[4,256,1024]{2,1,0:T(8,128)(2,1)} %bitcast.55, bf16[4,256,1024]{2,1,0:T(8,128)(2,1)} %bitcast.56, bf16[4,256,1024]{2,1,0:T(8,128)(2,1)} %bitcast.57, bf16[4,256,1024]{2,1,0:T(8,128)(2,1)} %bitcast.58, bf16[4096,3584]{1,0:T(8,128)(2,1)} %refs_4_.7, ...), custom_call_target="tpu_custom_call" | custom-call | flops 22548578304 | bytes 88080384 | tf_op jit(solution)/shard_map/pallas_call | solution.py:214
  454.4 37.8 %shard_map.149.refs_7_ = f32[4,256,1024]{2,1,0:T(8,128)} custom-call(s32[1]{0:T(128)} %bitcast.rank_ref, bf16[256,1024]{1,0:T(8,128)(2,1)} %multiply_convert_fusion.1.refs_7_.refs_0_, bf16[256,1024]{1,0:T(8,128)(2,1)} %copy-done.3, bf16[256,1024]{1,0:T(8,128)(2,1)} %collective-permute-done.20.refs_2_, bf16[256,1024]{1,0:T(8,128)(2,1)} %copy-done.4, ...), custom_call_target="tpu_custom_call" | custom-call | flops 22548578304 | bytes 88080384 | tf_op jit(solution)/shard_map/pallas_call | solution.py:214
  495.5 32.4 %reduce-scatter.7.cloned.1.call-done = f32[1,256,1024]{2,1,0:T(8,128)} async-done(((f32[4,256,1024]{2,1,0:T(8,128)}), f32[1,256,1024]{2,1,0:T(8,128)}) %reduce-scatter.7.cloned.1.call-update) | async-done | bytes 1048592 | tf_op jit(solution)/shard_map/reduce_scatter | solution.py:369
  531.6 37.4 %shard_map.150 = f32[4,256,1024]{2,1,0:T(8,128)} custom-call(s32[1]{0:T(128)} %bitcast.rank_ref, bf16[256,1024]{1,0:T(8,128)(2,1)} %multiply_convert_fusion.refs_7_.refs_0_, bf16[256,1024]{1,0:T(8,128)(2,1)} %copy-done.6, bf16[256,1024]{1,0:T(8,128)(2,1)} %collective-permute-done.18.refs_2_, bf16[256,1024]{1,0:T(8,128)(2,1)} %copy-done.8, ...), custom_call_target="tpu_custom_call" | custom-call | flops 22548578304 | bytes 88080384 | tf_op jit(solution)/shard_map/pallas_call | solution.py:214
  572.1 27.3 %reduce-scatter.11.cloned.1.call-done = f32[1,256,1024]{2,1,0:T(8,128)} async-done(((f32[4,256,1024]{2,1,0:T(8,128)}), f32[1,256,1024]{2,1,0:T(8,128)}) %reduce-scatter.11.cloned.1.call-update) | async-done | bytes 1048592 | tf_op jit(solution)/shard_map/reduce_scatter | solution.py:369
  601.6 70.9 %reduce-scatter.9.cloned.1.call-done = f32[1,256,1024]{2,1,0:T(8,128)} async-done(((f32[4,256,1024]{2,1,0:T(8,128)}), f32[1,256,1024]{2,1,0:T(8,128)}) %reduce-scatter.9.cloned.1.call-update) | async-done | bytes 1048592 | tf_op jit(solution)/shard_map/reduce_scatter | solution.py:369
  678.1 10.6 %collective-permute-done.23.refs_1_ = bf16[256,1024]{1,0:T(8,128)(2,1)S(1)} collective-permute-done((bf16[256,1024]{1,0:T(8,128)(2,1)S(1)}, bf16[256,1024]{1,0:T(8,128)(2,1)S(1)}, u32[]{:S(2)}, u32[]{:S(2)}) %collective-permute-start.23) | collective-permute-done | bytes 524320 | tf_op jit(solution)/shard_map/ppermute | solution.py:268
  703.0 8.2 %collective-permute-done.26.refs_1_ = bf16[256,1024]{1,0:T(8,128)(2,1)S(1)} collective-permute-done((bf16[256,1024]{1,0:T(8,128)(2,1)}, bf16[256,1024]{1,0:T(8,128)(2,1)S(1)}, u32[]{:S(2)}, u32[]{:S(2)}) %collective-permute-start.26) | collective-permute-done | bytes 524320 | tf_op jit(solution)/shard_map/ppermute | solution.py:268
  (228 shorter events, 175.5 us)
Async XLA Ops:
  7.2 88.8 %all-gather.8.cloned.1.call-start = ((), (), s32[]{:S(2)}) async-start(), calls=%async_computation.4 | async-start | bytes 9437184 | tf_op jit(solution)/shard_map/all_gather | solution.py:318
  26.8 180.0 %all-gather.10.cloned.1.call-start = ((), (), s32[]{:S(2)}) async-start(), calls=%async_computation.9 | async-start | bytes 9437184 | tf_op jit(solution)/shard_map/all_gather | solution.py:331
  48.1 275.4 %all-gather.12.cloned.1.call-start = ((), (), s32[]{:S(2)}) async-start(), calls=%async_computation.10 | async-start | bytes 2621440 | tf_op jit(solution)/shard_map/all_gather | solution.py:356
  130.8 38.3 %collective-permute-start = (bf16[256,1024]{1,0:T(8,128)(2,1)}, bf16[256,1024]{1,0:T(8,128)(2,1)S(1)}, u32[]{:S(2)}, u32[]{:S(2)}) collective-permute-start(bf16[256,1024]{1,0:T(8,128)(2,1)} %shard_map.139.refs_0_), channel_id=1, source_target_pairs={{0,24},{8,0},{16,8},{24,16},{1,25},{9,1},{17,9},{25,17},{2,26},{10... | collective-permute-start | bytes 1572872 | tf_op jit(solution)/shard_map/ppermute | solution.py:268
  133.1 34.9 %collective-permute-start.1 = (bf16[256,1024]{1,0:T(8,128)(2,1)}, bf16[256,1024]{1,0:T(8,128)(2,1)S(1)}, u32[]{:S(2)}, u32[]{:S(2)}) collective-permute-start(bf16[256,1024]{1,0:T(8,128)(2,1)} %shard_map.139.refs_0_), channel_id=1, source_target_pairs={{0,8},{8,16},{16,24},{24,0},{1,9},{9,17},{17,25},{25,1},{2,10},{10... | collective-permute-start | bytes 1572872 | tf_op jit(solution)/shard_map/ppermute | solution.py:268
  168.0 38.8 %collective-permute-start.2 = (bf16[256,1024]{1,0:T(8,128)(2,1)S(1)}, bf16[256,1024]{1,0:T(8,128)(2,1)S(1)}, u32[]{:S(2)}, u32[]{:S(2)}) collective-permute-start(bf16[256,1024]{1,0:T(8,128)(2,1)S(1)} %collective-permute-done.1.refs_2_.refs_3_), channel_id=1, source_target_pairs={{0,8},{8,16},{16,24},{24,0},{1,9},{9,17},{17,25},{25,1},{2,10},{10... | collective-permute-start | bytes 1572872 | tf_op jit(solution)/shard_map/ppermute | solution.py:268
  228.8 170.2 %all-gather.14.cloned.1.call-start = ((), (), s32[]{:S(2)}) async-start(), calls=%async_computation.11 | async-start | bytes 2621440 | tf_op jit(solution)/shard_map/all_gather | solution.py:356
  232.8 69.5 %collective-permute-start.11 = (bf16[256,1024]{1,0:T(8,128)(2,1)S(1)}, bf16[256,1024]{1,0:T(8,128)(2,1)S(1)}, u32[]{:S(2)}, u32[]{:S(2)}) collective-permute-start(bf16[256,1024]{1,0:T(8,128)(2,1)S(1)} %copy-done.24), channel_id=1, source_target_pairs={{0,24},{8,0},{16,8},{24,16},{1,25},{9,1},{17,9},{25,17},{2,26},{10... | collective-permute-start | bytes 1572872 | tf_op jit(solution)/shard_map/ppermute | solution.py:268
  234.1 51.3 %collective-permute-start.12 = (bf16[256,1024]{1,0:T(8,128)(2,1)S(1)}, bf16[256,1024]{1,0:T(8,128)(2,1)S(1)}, u32[]{:S(2)}, u32[]{:S(2)}) collective-permute-start(bf16[256,1024]{1,0:T(8,128)(2,1)S(1)} %copy-done.24), channel_id=1, source_target_pairs={{0,8},{8,16},{16,24},{24,0},{1,9},{9,17},{17,25},{25,1},{2,10},{10... | collective-permute-start | bytes 1572872 | tf_op jit(solution)/shard_map/ppermute | solution.py:268
  238.2 39.1 %collective-permute-start.14 = (bf16[256,1024]{1,0:T(8,128)(2,1)S(1)}, bf16[256,1024]{1,0:T(8,128)(2,1)}, u32[]{:S(2)}, u32[]{:S(2)}) collective-permute-start(bf16[256,1024]{1,0:T(8,128)(2,1)S(1)} %collective-permute-done.6.refs_1_), channel_id=1, source_target_pairs={{0,24},{8,0},{16,8},{24,16},{1,25},{9,1},{17,9},{25,17},{2,26},{10... | collective-permute-start | bytes 1572872 | tf_op jit(solution)/shard_map/ppermute | solution.py:268
  299.7 141.3 %reduce-scatter.5.cloned.1.call-start = ((), (), s32[]{:S(2)}) async-start(), calls=%async_computation.5 | async-start | bytes 5242880 | tf_op jit(solution)/shard_map/reduce_scatter | solution.py:369
  362.1 165.7 %reduce-scatter.7.cloned.1.call-start = ((), (), s32[]{:S(2)}) async-start(), calls=%async_computation.6 | async-start | bytes 5242880 | tf_op jit(solution)/shard_map/reduce_scatter | solution.py:369
  436.6 162.7 %reduce-scatter.11.cloned.1.call-start = ((), (), s32[]{:S(2)}) async-start(), calls=%async_computation.8 | async-start | bytes 5242880 | tf_op jit(solution)/shard_map/reduce_scatter | solution.py:369
  492.3 180.1 %reduce-scatter.9.cloned.1.call-start = ((), (), s32[]{:S(2)}) async-start(), calls=%async_computation.7 | async-start | bytes 5242880 | tf_op jit(solution)/shard_map/reduce_scatter | solution.py:369
  493.3 36.7 %collective-permute-start.18 = (bf16[256,1024]{1,0:T(8,128)(2,1)S(1)}, bf16[256,1024]{1,0:T(8,128)(2,1)}, u32[]{:S(2)}, u32[]{:S(2)}) collective-permute-start(bf16[256,1024]{1,0:T(8,128)(2,1)S(1)} %copy-done.7), channel_id=1, source_target_pairs={{0,24},{8,0},{16,8},{24,16},{1,25},{9,1},{17,9},{25,17},{2,26},{10... | collective-permute-start | bytes 1572872 | tf_op jit(solution)/shard_map/ppermute | solution.py:268
  493.4 36.6 %collective-permute-start.21 = (bf16[256,1024]{1,0:T(8,128)(2,1)S(1)}, bf16[256,1024]{1,0:T(8,128)(2,1)S(1)}, u32[]{:S(2)}, u32[]{:S(2)}) collective-permute-start(bf16[256,1024]{1,0:T(8,128)(2,1)S(1)} %copy-done.12), channel_id=1, source_target_pairs={{0,24},{8,0},{16,8},{24,16},{1,25},{9,1},{17,9},{25,17},{2,26},{10... | collective-permute-start | bytes 1572872 | tf_op jit(solution)/shard_map/ppermute | solution.py:268
  493.4 36.6 %collective-permute-start.22 = (bf16[256,1024]{1,0:T(8,128)(2,1)S(1)}, bf16[256,1024]{1,0:T(8,128)(2,1)S(1)}, u32[]{:S(2)}, u32[]{:S(2)}) collective-permute-start(bf16[256,1024]{1,0:T(8,128)(2,1)S(1)} %copy-done.12), channel_id=1, source_target_pairs={{0,8},{8,16},{16,24},{24,0},{1,9},{9,17},{17,25},{25,1},{2,10},{10... | collective-permute-start | bytes 1572872 | tf_op jit(solution)/shard_map/ppermute | solution.py:268
  570.0 103.9 %collective-permute-start.29 = (bf16[256,1024]{1,0:T(8,128)(2,1)S(1)}, bf16[256,1024]{1,0:T(8,128)(2,1)}, u32[]{:S(2)}, u32[]{:S(2)}) collective-permute-start(bf16[256,1024]{1,0:T(8,128)(2,1)S(1)} %copy-done.11), channel_id=1, source_target_pairs={{0,24},{8,0},{16,8},{24,16},{1,25},{9,1},{17,9},{25,17},{2,26},{10... | collective-permute-start | bytes 1572872 | tf_op jit(solution)/shard_map/ppermute | solution.py:268
  571.7 103.5 %collective-permute-start.31 = (bf16[256,1024]{1,0:T(8,128)(2,1)S(1)}, bf16[256,1024]{1,0:T(8,128)(2,1)}, u32[]{:S(2)}, u32[]{:S(2)}) collective-permute-start(bf16[256,1024]{1,0:T(8,128)(2,1)S(1)} %copy-done.11), channel_id=1, source_target_pairs={{0,8},{8,16},{16,24},{24,0},{1,9},{9,17},{17,25},{25,1},{2,10},{10... | collective-permute-start | bytes 1572872 | tf_op jit(solution)/shard_map/ppermute | solution.py:268
  572.1 104.9 %collective-permute-start.32 = (bf16[256,1024]{1,0:T(8,128)(2,1)S(1)}, bf16[256,1024]{1,0:T(8,128)(2,1)}, u32[]{:S(2)}, u32[]{:S(2)}) collective-permute-start(bf16[256,1024]{1,0:T(8,128)(2,1)S(1)} %copy-done.22), channel_id=1, source_target_pairs={{0,8},{8,16},{16,24},{24,0},{1,9},{9,17},{17,25},{25,1},{2,10},{10... | collective-permute-start | bytes 1572872 | tf_op jit(solution)/shard_map/ppermute | solution.py:268
  601.6 75.7 %collective-permute-start.27 = (bf16[256,1024]{1,0:T(8,128)(2,1)}, bf16[256,1024]{1,0:T(8,128)(2,1)S(1)}, u32[]{:S(2)}, u32[]{:S(2)}) collective-permute-start(bf16[256,1024]{1,0:T(8,128)(2,1)} %fusion.3.refs_0_), channel_id=1, source_target_pairs={{0,8},{8,16},{16,24},{24,0},{1,9},{9,17},{17,25},{25,1},{2,10},{10... | collective-permute-start | bytes 1572872 | tf_op jit(solution)/shard_map/ppermute | solution.py:268
  675.2 36.0 %collective-permute-start.26 = (bf16[256,1024]{1,0:T(8,128)(2,1)}, bf16[256,1024]{1,0:T(8,128)(2,1)S(1)}, u32[]{:S(2)}, u32[]{:S(2)}) collective-permute-start(bf16[256,1024]{1,0:T(8,128)(2,1)} %fusion.3.refs_0_), channel_id=1, source_target_pairs={{0,24},{8,0},{16,8},{24,16},{1,25},{9,1},{17,9},{25,17},{2,26},{10... | collective-permute-start | bytes 1572872 | tf_op jit(solution)/shard_map/ppermute | solution.py:268
  676.9 38.8 %collective-permute-start.25 = (bf16[256,1024]{1,0:T(8,128)(2,1)S(1)}, bf16[256,1024]{1,0:T(8,128)(2,1)S(1)}, u32[]{:S(2)}, u32[]{:S(2)}) collective-permute-start(bf16[256,1024]{1,0:T(8,128)(2,1)S(1)} %fusion.4.refs_0_), channel_id=1, source_target_pairs={{0,8},{8,16},{16,24},{24,0},{1,9},{9,17},{17,25},{25,1},{2,10},{10... | collective-permute-start | bytes 1572872 | tf_op jit(solution)/shard_map/ppermute | solution.py:268
  677.2 33.9 %collective-permute-start.28 = (bf16[256,1024]{1,0:T(8,128)(2,1)S(1)}, bf16[256,1024]{1,0:T(8,128)(2,1)S(1)}, u32[]{:S(2)}, u32[]{:S(2)}) collective-permute-start(bf16[256,1024]{1,0:T(8,128)(2,1)S(1)} %collective-permute-done.27.refs_3_), channel_id=1, source_target_pairs={{0,8},{8,16},{16,24},{24,0},{1,9},{9,17},{17,25},{25,1},{2,10},{10... | collective-permute-start | bytes 1572872 | tf_op jit(solution)/shard_map/ppermute | solution.py:268
  (63 other events, 677.4 us)
Sparse Core Ops, SparseCore 0:
  26.9 48.1 all-gather.7
  76.7 47.2 all-gather.9
  228.9 49.1 all-gather.11
  299.8 50.8 all-gather.13
  362.2 70.3 reduce-scatter.4
  436.7 91.0 reduce-scatter.6
  530.7 68.6 reduce-scatter.10
  601.7 70.7 reduce-scatter.8

commit v3 on v2

--- a/solution.py
+++ b/solution.py
@@ -43,11 +43,11 @@
     return jnp.concatenate([t_lo * cos_t - t_hi * sin_t, t_hi * cos_t + t_lo * sin_t], axis=-1)
 
 
-def attn_kernel(group, bounds_ref, q_ref, k_ref, v_ref, first_ref, *refs):
+def attn_kernel(group, chunk, bounds_ref, q_ref, k_ref, v_ref, first_ref, *refs):
     o_ref, q_scr, m_scr, l_scr, acc_scr = refs[-5:]
     rows = q_ref.shape[0]
     block = min(KV_BLOCK, k_ref.shape[0])
-    row0, first_lo, first_hi = bounds_ref[0], bounds_ref[1], bounds_ref[2]
+    row0, first_lo, first_hi = bounds_ref[3 * chunk], bounds_ref[3 * chunk + 1], bounds_ref[3 * chunk + 2]
     m_scr[...] = jnp.full_like(m_scr, MASKED)
     l_scr[...] = jnp.zeros_like(l_scr)
     acc_scr[...] = jnp.zeros_like(acc_scr)
@@ -105,7 +105,7 @@
     group = width // HEAD_DIM
     flops = 4 * rows * q_rot.shape[1] * tokens
     return pl.pallas_call(
-        functools.partial(attn_kernel, group),
+        functools.partial(attn_kernel, group, chunk),
         out_shape=jax.ShapeDtypeStruct((rows, q_rot.shape[1]), BF16),
         grid_spec=pltpu.PrefetchScalarGridSpec(
             num_scalar_prefetch=1,
@@ -276,10 +276,9 @@
 
 
 def pipeline_order(chunks):
-    order = [("attn", 0), ("attn", 1)]
-    for chunk in range(2, chunks):
-        order += [("attn", chunk), ("out", chunk - 2)]
-    order += [("out", chunks - 2), ("mlp", 0), ("out", chunks - 1)]
+    order = [("attn", chunk) for chunk in range(chunks - 1)]
+    order += [("out", chunk) for chunk in range(chunks - 2)]
+    order += [("attn", chunks - 1), ("mlp", 0), ("out", chunks - 2), ("out", chunks - 1)]
     return order + [("mlp", chunk) for chunk in range(1, chunks)]
 
 
@@ -316,7 +315,8 @@
         v_proj = jnp.dot(u_norm, w_v, preferred_element_type=F32).astype(BF16)
         kv_own = jnp.concatenate([k_rot.reshape(rows_local, -1), v_proj], axis=1)
         kv_all = lax.all_gather(kv_own, "sp", tiled=True)
-        q_rot = rotate(jnp.dot(u_norm, w_q, preferred_element_type=F32).reshape(rows_local, -1, HEAD_DIM), cos_t, sin_t).astype(BF16)
+        q_raw = jnp.dot(u_norm, w_q, preferred_element_type=F32)
+        q_rot = rotate(q_raw.reshape(rows_local, -1, HEAD_DIM), cos_t, sin_t).astype(BF16)
         q_rot = q_rot.reshape(rows_local, -1)
         slot_head = sp_rank // kv_repeat
         k_cache = lax.dynamic_slice_in_dim(kv_all, slot_head * HEAD_DIM, HEAD_DIM, axis=1)[:, None, :]
@@ -334,37 +334,51 @@
 
         rank = jnp.reshape(tp_rank, (1,)).astype(jnp.int32)
         rank_zero = jnp.zeros((1,), jnp.int32)
-        attn_all, x_mid, u_all, y_own, y_all = {}, {}, {}, {}, {}
+        bounds = jnp.stack([row_base + chunk * rows + jnp.zeros((), jnp.int32) if part == 0 else
+                            first_rows[chunk * rows + (part - 1) * (rows - 1)]
+                            for chunk in range(CHUNKS) for part in range(3)])
+
+        def near(parts):
+            return [parts[1], parts[-1]]
+
+        attn_all, x_mid, u_all, y_own, y_all, row_sq = {}, {}, {}, {}, {}, {}
         after = [q_rot]
         for stage, chunk in pipeline_order(CHUNKS):
-            row0 = chunk * rows
             forward = chunk % 2 == 0
             if stage == "attn":
                 if chunk >= 2:
-                    after = after + [attn_all[chunk - 2][1], attn_all[chunk - 2][-1]]
-                bounds = jnp.stack([row_base + row0, first_rows[row0], first_rows[row0 + rows - 1]])
+                    after = after + near(attn_all[chunk - 2])
                 attn_own = attention_chunk(bounds, q_rot, kv_all, first_rows[None, :], chunk, rows, kv_local, after)
                 attn_all[chunk] = ring_gather(attn_own, "tp", tp_size, forward)
                 after = [attn_own]
             elif stage == "out":
-                if chunk == CHUNKS - 1 and CHUNKS >= 4 and tp_size == 4:
-                    after = after + [u_all[2][1], u_all[2][-1]]
+                if chunk == CHUNKS - 2:
+                    after = after + near(attn_all[CHUNKS - 1])
                 x_mid[chunk], ssq = out_proj(attn_all[chunk], wo_cols, x_cols, chunk, after)
-                sum_sq = lax.psum(jnp.sum(ssq, axis=1), "tp")
-                u_own = (x_mid[chunk] * lax.rsqrt(sum_sq[:, None] / model + NORM_EPS) * gain_cols).astype(BF16)
-                on_queue = chunk < 2
-                u_all[chunk] = lax.all_gather(u_own, "tp") if on_queue else ring_gather(u_own, "tp", tp_size, forward)
-                after = [u_own]
+                row_sq[chunk] = jnp.sum(ssq, axis=1)
+                after = [x_mid[chunk]]
+                if chunk % 2 == 1:
+                    pair = (chunk - 1, chunk)
+                    sums = lax.psum(jnp.concatenate([row_sq[c] for c in pair]), "tp")
+                    after = []
+                    for place, c in enumerate(pair):
+                        sum_sq = sums[place * rows:(place + 1) * rows]
+                        u_own = (x_mid[c] * lax.rsqrt(sum_sq[:, None] / model + NORM_EPS) * gain_cols).astype(BF16)
+                        if c == 0:
+                            u_all[c] = lax.all_gather(u_own, "tp")
+                        else:
+                            u_all[c] = ring_gather(u_own, "tp", tp_size, c % 2 == 0)
+                        after.append(u_own)
             else:
+                if chunk == 0:
+                    after = after + near(u_all[1]) + near(attn_all[CHUNKS - 2])
                 if chunk >= 2:
-                    after = after + [u_all[chunk][1], u_all[chunk][-1], y_own[chunk - 2]]
-                if chunk + 1 < CHUNKS and isinstance(u_all[chunk + 1], list):
-                    after = after + [u_all[chunk + 1][1], u_all[chunk + 1][-1]]
+                    after = after + [y_own[chunk - 2]]
+                    if chunk + 1 < CHUNKS:
+                        after = after + near(u_all[chunk + 1])
                 if chunk >= 3:
-                    after = after + [y_all[chunk - 3][1], y_all[chunk - 3][-1]]
+                    after = after + near(y_all[chunk - 3])
                 own_rank = rank if isinstance(u_all[chunk], list) else rank_zero
-                if chunk == 0:
-                    after = after + [attn_all[CHUNKS - 1][1], attn_all[CHUNKS - 1][-1]]
                 partial = mlp_partial(own_rank, u_all[chunk], w_gate, w_up, w_down, after)
                 down = lax.psum_scatter(partial, "tp", scatter_dimension=0, tiled=False)
                 y_own[chunk] = (x_mid[chunk] + down).astype(BF16)

time: 741 us -> 747 us (level)
  waiting for transfers between devices: 195 us -> 225 us
  blocking collectives: 48.7 us -> 30.6 us
  other arithmetic: 45.6 us -> 32.4 us
    psum x4 -> x2, blocking collectives: 41.2 us -> 23.1 us  [local_layer(): sums = lax.psum(jnp.concatenate([row_sq[c] for c in pair]), 'tp')]
    reduce_scatter x4, waiting for transfers between devices: 131 us -> 149 us  [local_layer(): down = lax.psum_scatter(partial, 'tp', scatter_dimension=0, tiled=False)]
    another operation x6 -> x2, other arithmetic: 12.8 us -> 5.17 us  [the longest x4 7.62 us: local_layer(): jnp.stack([row_base + row0, first_rows[row0], first_rows[row0 + rows - 1]])]
    ppermute x30 -> x33, starting transfers between devices: 27.3 us -> 33.9 us  [shifted(): lax.ppermute(block, axis, [(i, (i + shift) % size) for i in range(size)])]
    ppermute x30 -> x33, waiting for transfers between devices: 53.6 us -> 58.4 us  [shifted(): lax.ppermute(block, axis, [(i, (i + shift) % size) for i in range(size)])]
    unnamed x98 -> x88, local copies, waits for them, and re-layouts: 24.7 us -> 20.1 us
  transfers between devices with their start and end apart: 41 -> 43, of which waited for: 14 -> 16; matrix products, arithmetic and copies ran while one was open for 9% -> 8% of each run, Pallas kernels for 44% -> 39%
where the time goes in v3:
time: 747 us; the launch traced here: 737 us
  Pallas kernels  334 us (45%)
  waiting for transfers between devices  225 us (30%)
  starting transfers between devices  41.6 us (6%)
  local copies, waits for them, and re-layouts  38.5 us (5%)
  other arithmetic  32.4 us (4%)
  blocking collectives  30.6 us (4%)
  matrix products  20.4 us (3%)
  between operations  15.1 us (2%)
    pallas_call x4, Pallas kernels, mlp_partial(): pl.pallas_call(functools.partial(mlp_kernel, parts), out_shape=jax.ShapeD...  149 us
    reduce_scatter x4, waiting for transfers between devices, local_layer(): down = lax.psum_scatter(partial, 'tp', scatter_dimension=0, tiled=False)  149 us
    pallas_call x4, Pallas kernels, attention_chunk(): pl.pallas_call(functools.partial(attn_kernel, group, chunk), out_shape=ja...  144 us
    ppermute x33, waiting for transfers between devices, shifted(): lax.ppermute(block, axis, [(i, (i + shift) % size) for i in range(size)])  58.4 us
    ppermute x33, starting transfers between devices, shifted(): lax.ppermute(block, axis, [(i, (i + shift) % size) for i in range(size)])  33.9 us
    pallas_call x4, Pallas kernels, out_proj(): pl.pallas_call(functools.partial(out_proj_kernel, parts), out_shape=(jax....  28.8 us
    psum x2, blocking collectives, local_layer(): sums = lax.psum(jnp.concatenate([row_sq[c] for c in pair]), 'tp')  23.1 us
    unnamed x88, local copies, waits for them, and re-layouts  20.1 us
  transfers between devices with their start and end apart: 43, of which 16 were waited for; matrix products, arithmetic and copies ran while one was open for 8% of the time, Pallas kernels for 39%

profile of v3, /device:TPU:102, one launch (start us, length us, event | category | flops | bytes accessed | tf_op | source)
XLA Modules:
  0.0 737.3 jit_solution(2615460040920219956)
XLA Ops:
  40.1 6.8 collective-permute-done.4
  48.3 7.5 %psum.21 = s32[2]{0:T(128)S(1)} all-reduce(s32[2]{0:T(128)S(1)} %fusion.8), channel_id=1, replica_groups=mesh['rep'=1,'tp'=4,'sp'=8] {'sp'}, use_global_device_ids=true, to_apply=%region_1.0 | all-reduce | flops 2 | bytes 16 | tf_op jit(solution)/shard_map/psum | solution.py:307
  55.8 14.2 %fusion.12 = f32[1024,1024]{0,1:T(8,128)S(1)} fusion(bf16[4096,1024]{1,0:T(8,128)(2,1)} %param.16, bf16[1024,4096]{1,0:T(8,128)(2,1)} %param.12, f32[4096]{0:T(1024)S(1)} %copy-done.40, f32[1024]{0:T(1024)S(1)} %add_rsqrt_fusion), kind=kOutput, calls=%fused_computation.47 | convolution fusion | flops 8606711808 | bytes 20992000 | tf_op jit(solution)/shard_map/dot_general | solution.py:318
  92.0 34.7 %shard_map.139.refs_0_ = bf16[256,1024]{1,0:T(8,128)(2,1)} custom-call(s32[12]{0:T(128)} %stack.34.bounds_ref, bf16[1024,1024]{1,0:T(8,128)(2,1)} %bitcast.57, bf16[8192,512]{1,0:T(8,128)(2,1)} %all-gather.6.cloned.1.call-done.k_ref.v_ref, bf16[8192,512]{1,0:T(8,128)(2,1)} %all-gather.6.cloned.1.call-done.k_ref.v_ref, s32[1,1024]{1,0:T(1,128)} %bitcast.67, ...), custom_call_target="tpu_custom_call" | custom-call | flops 17179869184 | bytes 8388608 | tf_op jit(solution)/shard_map/pallas_call | solution.py:107
  126.7 35.4 %shard_map.140.refs_0_ = bf16[256,1024]{1,0:T(8,128)(2,1)} custom-call(s32[12]{0:T(128)} %stack.34.bounds_ref, bf16[1024,1024]{1,0:T(8,128)(2,1)} %bitcast.59, bf16[8192,512]{1,0:T(8,128)(2,1)} %all-gather.6.cloned.1.call-done.k_ref.v_ref, bf16[8192,512]{1,0:T(8,128)(2,1)} %all-gather.6.cloned.1.call-done.k_ref.v_ref, s32[1,1024]{1,0:T(1,128)} %bitcast.68, ...), custom_call_target="tpu_custom_call" | custom-call | flops 17179869184 | bytes 8388608 | tf_op jit(solution)/shard_map/pallas_call | solution.py:107
  182.4 36.9 %shard_map.141.refs_6_.refs_0_ = bf16[256,1024]{1,0:T(8,128)(2,1)} custom-call(s32[12]{0:T(128)} %stack.34.bounds_ref, bf16[1024,1024]{1,0:T(8,128)(2,1)} %bitcast.60, bf16[8192,512]{1,0:T(8,128)(2,1)} %all-gather.6.cloned.1.call-done.k_ref.v_ref, bf16[8192,512]{1,0:T(8,128)(2,1)} %all-gather.6.cloned.1.call-done.k_ref.v_ref, s32[1,1024]{1,0:T(1,128)} %bitcast.69, ...), custom_call_target="tpu_custom_call" | custom-call | flops 17179869184 | bytes 8388608 | tf_op jit(solution)/shard_map/pallas_call | solution.py:107
  220.2 7.0 shard_map.142
  228.1 7.2 shard_map.143
  236.4 11.3 %psum.22 = f32[512]{0:T(512)S(1)} all-reduce(f32[512]{0:T(512)S(1)} %pad_maximum_fusion.4), channel_id=1, replica_groups=mesh['rep'=1,'tp'=4,'sp'=8] {'tp'}, use_global_device_ids=true, to_apply=%region_6.7 | all-reduce | flops 512 | bytes 4096 | tf_op jit(solution)/shard_map/psum | solution.py:362
  254.4 37.1 %shard_map.144.refs_7_.refs_0_ = bf16[256,1024]{1,0:T(8,128)(2,1)} custom-call(s32[12]{0:T(128)} %stack.34.bounds_ref, bf16[1024,1024]{1,0:T(8,128)(2,1)} %bitcast.61, bf16[8192,512]{1,0:T(8,128)(2,1)} %all-gather.6.cloned.1.call-done.k_ref.v_ref, bf16[8192,512]{1,0:T(8,128)(2,1)} %all-gather.6.cloned.1.call-done.k_ref.v_ref, s32[1,1024]{1,0:T(1,128)} %bitcast.70, ...), custom_call_target="tpu_custom_call" | custom-call | flops 17179869184 | bytes 8388608 | tf_op jit(solution)/shard_map/pallas_call | solution.py:107
  291.6 6.8 all-gather.10.cloned.1.call-done
  298.4 36.9 %shard_map.145.refs_6_ = f32[4,256,1024]{2,1,0:T(8,128)} custom-call(s32[1]{0:T(128)} %constant.111.clone.1.rank_ref, bf16[4,256,1024]{2,1,0:T(8,128)(2,1)} %bitcast.50, bf16[4,256,1024]{2,1,0:T(8,128)(2,1)} %bitcast.51, bf16[4,256,1024]{2,1,0:T(8,128)(2,1)} %bitcast.52, bf16[4,256,1024]{2,1,0:T(8,128)(2,1)} %bitcast.53, bf16[4096,3584]{1,0:T(8,128)(2,1)} %refs_4_.7, ...), custom_call_target="tpu_custom_call" | custom-call | flops 22548578304 | bytes 88080384 | tf_op jit(solution)/shard_map/pallas_call | solution.py:214
  338.8 6.7 collective-permute-done.9.refs_7_.refs_1_
  352.7 7.3 shard_map.146
  360.0 7.3 shard_map.147
  368.4 11.8 %psum.23 = f32[512]{0:T(512)S(1)} all-reduce(f32[512]{0:T(512)S(1)} %pad_maximum_fusion.5), channel_id=1, replica_groups=mesh['rep'=1,'tp'=4,'sp'=8] {'tp'}, use_global_device_ids=true, to_apply=%region_9.10 | all-reduce | flops 512 | bytes 4096 | tf_op jit(solution)/shard_map/psum | solution.py:362
  382.7 37.4 %shard_map.148.refs_7_ = f32[4,256,1024]{2,1,0:T(8,128)} custom-call(s32[1]{0:T(128)} %bitcast.rank_ref, bf16[256,1024]{1,0:T(8,128)(2,1)} %get-tuple-element.37.refs_1_.refs_0_, bf16[256,1024]{1,0:T(8,128)(2,1)} %copy-done.11, bf16[256,1024]{1,0:T(8,128)(2,1)} %collective-permute-done.23.refs_2_, bf16[256,1024]{1,0:T(8,128)(2,1)} %copy-done.13, ...), custom_call_target="tpu_custom_call" | custom-call | flops 22548578304 | bytes 88080384 | tf_op jit(solution)/shard_map/pallas_call | solution.py:214
  442.9 37.3 %shard_map.149.refs_7_ = f32[4,256,1024]{2,1,0:T(8,128)} custom-call(s32[1]{0:T(128)} %bitcast.rank_ref, bf16[256,1024]{1,0:T(8,128)(2,1)} %get-tuple-element.35.refs_7_.refs_0_, bf16[256,1024]{1,0:T(8,128)(2,1)} %collective-permute-done.20.refs_1_, bf16[256,1024]{1,0:T(8,128)(2,1)} %collective-permute-done.22.refs_2_, ...), custom_call_target="tpu_custom_call" | custom-call | flops 22548578304 | bytes 88080384 | tf_op jit(solution)/shard_map/pallas_call | solution.py:214
  483.3 33.0 %reduce-scatter.7.cloned.1.call-done = f32[1,256,1024]{2,1,0:T(8,128)} async-done(((f32[4,256,1024]{2,1,0:T(8,128)}), f32[1,256,1024]{2,1,0:T(8,128)}) %reduce-scatter.7.cloned.1.call-update) | async-done | bytes 1048592 | tf_op jit(solution)/shard_map/reduce_scatter | solution.py:383
  519.2 37.2 %shard_map.150 = f32[4,256,1024]{2,1,0:T(8,128)} custom-call(s32[1]{0:T(128)} %bitcast.rank_ref, bf16[256,1024]{1,0:T(8,128)(2,1)} %get-tuple-element.36.refs_8_.refs_0_, bf16[256,1024]{1,0:T(8,128)(2,1)} %collective-permute-done.17.refs_9_.refs_1_, bf16[256,1024]{1,0:T(8,128)(2,1)} %collective-permute-done.18.refs_2_, ...), custom_call_target="tpu_custom_call" | custom-call | flops 22548578304 | bytes 88080384 | tf_op jit(solution)/shard_map/pallas_call | solution.py:214
  559.5 43.9 %reduce-scatter.11.cloned.1.call-done = f32[1,256,1024]{2,1,0:T(8,128)} async-done(((f32[4,256,1024]{2,1,0:T(8,128)}), f32[1,256,1024]{2,1,0:T(8,128)}) %reduce-scatter.11.cloned.1.call-update) | async-done | bytes 1048592 | tf_op jit(solution)/shard_map/reduce_scatter | solution.py:383
  606.1 71.7 %reduce-scatter.9.cloned.1.call-done = f32[1,256,1024]{2,1,0:T(8,128)} async-done(((f32[4,256,1024]{2,1,0:T(8,128)}), f32[1,256,1024]{2,1,0:T(8,128)}) %reduce-scatter.9.cloned.1.call-update) | async-done | bytes 1048592 | tf_op jit(solution)/shard_map/reduce_scatter | solution.py:383
  683.5 10.6 %collective-permute-done.26.refs_1_ = bf16[256,1024]{1,0:T(8,128)(2,1)S(1)} collective-permute-done((bf16[256,1024]{1,0:T(8,128)(2,1)S(1)}, bf16[256,1024]{1,0:T(8,128)(2,1)S(1)}, u32[]{:S(2)}, u32[]{:S(2)}) %collective-permute-start.26) | collective-permute-done | bytes 524320 | tf_op jit(solution)/shard_map/ppermute | solution.py:268
  709.0 7.5 %collective-permute-done.29.refs_1_ = bf16[256,1024]{1,0:T(8,128)(2,1)S(1)} collective-permute-done((bf16[256,1024]{1,0:T(8,128)(2,1)}, bf16[256,1024]{1,0:T(8,128)(2,1)S(1)}, u32[]{:S(2)}, u32[]{:S(2)}) %collective-permute-start.29) | collective-permute-done | bytes 524320 | tf_op jit(solution)/shard_map/ppermute | solution.py:268
  (214 shorter events, 168.8 us)
Async XLA Ops:
  7.2 84.8 %all-gather.6.cloned.1.call-start = ((), (), s32[]{:S(2)}) async-start(), calls=%async_computation.4 | async-start | bytes 9437184 | tf_op jit(solution)/shard_map/all_gather | solution.py:317
  26.8 192.6 %all-gather.8.cloned.1.call-start = ((), (), s32[]{:S(2)}) async-start(), calls=%async_computation.9 | async-start | bytes 9437184 | tf_op jit(solution)/shard_map/all_gather | solution.py:331
  48.1 250.3 %all-gather.10.cloned.1.call-start = ((), (), s32[]{:S(2)}) async-start(), calls=%async_computation.10 | async-start | bytes 2621440 | tf_op jit(solution)/shard_map/all_gather | solution.py:368
  171.4 55.8 %collective-permute-start.8 = (bf16[256,1024]{1,0:T(8,128)(2,1)}, bf16[256,1024]{1,0:T(8,128)(2,1)S(1)}, u32[]{:S(2)}, u32[]{:S(2)}) collective-permute-start(bf16[256,1024]{1,0:T(8,128)(2,1)} %shard_map.140.refs_0_), channel_id=1, source_target_pairs={{0,8},{8,16},{16,24},{24,0},{1,9},{9,17},{17,25},{25,1},{2,10},{10... | collective-permute-start | bytes 1572872 | tf_op jit(solution)/shard_map/ppermute | solution.py:268
  171.5 55.8 %collective-permute-start.7 = (bf16[256,1024]{1,0:T(8,128)(2,1)S(1)}, bf16[256,1024]{1,0:T(8,128)(2,1)}, u32[]{:S(2)}, u32[]{:S(2)}) collective-permute-start(bf16[256,1024]{1,0:T(8,128)(2,1)S(1)} %collective-permute-done.6.refs_1_.refs_2_), channel_id=1, source_target_pairs={{0,24},{8,0},{16,8},{24,16},{1,25},{9,1},{17,9},{25,17},{2,26},{10... | collective-permute-start | bytes 1572872 | tf_op jit(solution)/shard_map/ppermute | solution.py:268
  175.0 44.3 %collective-permute-start.2 = (bf16[256,1024]{1,0:T(8,128)(2,1)S(1)}, bf16[256,1024]{1,0:T(8,128)(2,1)S(1)}, u32[]{:S(2)}, u32[]{:S(2)}) collective-permute-start(bf16[256,1024]{1,0:T(8,128)(2,1)S(1)} %collective-permute-done.1.refs_2_.refs_3_), channel_id=1, source_target_pairs={{0,8},{8,16},{16,24},{24,0},{1,9},{9,17},{17,25},{25,1},{2,10},{10... | collective-permute-start | bytes 1572872 | tf_op jit(solution)/shard_map/ppermute | solution.py:268
  250.2 181.5 %reduce-scatter.5.cloned.1.call-start = ((), (), s32[]{:S(2)}) async-start(), calls=%async_computation.5 | async-start | bytes 5242880 | tf_op jit(solution)/shard_map/reduce_scatter | solution.py:383
  250.3 41.2 %collective-permute-start.12 = (bf16[256,1024]{1,0:T(8,128)(2,1)}, bf16[256,1024]{1,0:T(8,128)(2,1)S(1)}, u32[]{:S(2)}, u32[]{:S(2)}) collective-permute-start(bf16[256,1024]{1,0:T(8,128)(2,1)} %shard_map.141.refs_6_.refs_0_), channel_id=1, source_target_pairs={{0,24},{8,0},{16,8},{24,16},{1,25},{9,1},{17,9},{25,17},{2,26},{10... | collective-permute-start | bytes 1572872 | tf_op jit(solution)/shard_map/ppermute | solution.py:268
  250.4 41.1 %collective-permute-start.13 = (bf16[256,1024]{1,0:T(8,128)(2,1)}, bf16[256,1024]{1,0:T(8,128)(2,1)S(1)}, u32[]{:S(2)}, u32[]{:S(2)}) collective-permute-start(bf16[256,1024]{1,0:T(8,128)(2,1)} %shard_map.141.refs_6_.refs_0_), channel_id=1, source_target_pairs={{0,8},{8,16},{16,24},{24,0},{1,9},{9,17},{17,25},{25,1},{2,10},{10... | collective-permute-start | bytes 1572872 | tf_op jit(solution)/shard_map/ppermute | solution.py:268
  252.4 39.1 %collective-permute-start.15 = (bf16[256,1024]{1,0:T(8,128)(2,1)}, bf16[256,1024]{1,0:T(8,128)(2,1)S(1)}, u32[]{:S(2)}, u32[]{:S(2)}) collective-permute-start(bf16[256,1024]{1,0:T(8,128)(2,1)} %get-tuple-element.37.refs_1_.refs_0_), channel_id=1, source_target_pairs={{0,24},{8,0},{16,8},{24,16},{1,25},{9,1},{17,9},{25,17},{2,26},{10... | collective-permute-start | bytes 1572872 | tf_op jit(solution)/shard_map/ppermute | solution.py:268
  253.7 37.8 %collective-permute-start.16 = (bf16[256,1024]{1,0:T(8,128)(2,1)}, bf16[256,1024]{1,0:T(8,128)(2,1)S(1)}, u32[]{:S(2)}, u32[]{:S(2)}) collective-permute-start(bf16[256,1024]{1,0:T(8,128)(2,1)} %get-tuple-element.37.refs_1_.refs_0_), channel_id=1, source_target_pairs={{0,8},{8,16},{16,24},{24,0},{1,9},{9,17},{17,25},{25,1},{2,10},{10... | collective-permute-start | bytes 1572872 | tf_op jit(solution)/shard_map/ppermute | solution.py:268
  335.4 180.9 %reduce-scatter.7.cloned.1.call-start = ((), (), s32[]{:S(2)}) async-start(), calls=%async_computation.6 | async-start | bytes 5242880 | tf_op jit(solution)/shard_map/reduce_scatter | solution.py:383
  346.9 35.8 %collective-permute-start.23 = (bf16[256,1024]{1,0:T(8,128)(2,1)S(1)}, bf16[256,1024]{1,0:T(8,128)(2,1)}, u32[]{:S(2)}, u32[]{:S(2)}) collective-permute-start(bf16[256,1024]{1,0:T(8,128)(2,1)S(1)} %copy-done.12), channel_id=1, source_target_pairs={{0,24},{8,0},{16,8},{24,16},{1,25},{9,1},{17,9},{25,17},{2,26},{10... | collective-permute-start | bytes 1572872 | tf_op jit(solution)/shard_map/ppermute | solution.py:268
  420.2 183.2 %reduce-scatter.11.cloned.1.call-start = ((), (), s32[]{:S(2)}) async-start(), calls=%async_computation.8 | async-start | bytes 5242880 | tf_op jit(solution)/shard_map/reduce_scatter | solution.py:383
  480.3 197.5 %reduce-scatter.9.cloned.1.call-start = ((), (), s32[]{:S(2)}) async-start(), calls=%async_computation.7 | async-start | bytes 5242880 | tf_op jit(solution)/shard_map/reduce_scatter | solution.py:383
  480.3 38.1 %collective-permute-start.18 = (bf16[256,1024]{1,0:T(8,128)(2,1)}, bf16[256,1024]{1,0:T(8,128)(2,1)}, u32[]{:S(2)}, u32[]{:S(2)}) collective-permute-start(bf16[256,1024]{1,0:T(8,128)(2,1)} %collective-permute-done.17.refs_9_.refs_1_), channel_id=1, source_target_pairs={{0,24},{8,0},{16,8},{24,16},{1,25},{9,1},{17,9},{25,17},{2,26},{10... | collective-permute-start | bytes 1572872 | tf_op jit(solution)/shard_map/ppermute | solution.py:268
  481.3 37.2 %collective-permute-start.24 = (bf16[256,1024]{1,0:T(8,128)(2,1)S(1)}, bf16[256,1024]{1,0:T(8,128)(2,1)S(1)}, u32[]{:S(2)}, u32[]{:S(2)}) collective-permute-start(bf16[256,1024]{1,0:T(8,128)(2,1)S(1)} %copy-done.8), channel_id=1, source_target_pairs={{0,24},{8,0},{16,8},{24,16},{1,25},{9,1},{17,9},{25,17},{2,26},{10... | collective-permute-start | bytes 1572872 | tf_op jit(solution)/shard_map/ppermute | solution.py:268
  481.3 37.2 %collective-permute-start.25 = (bf16[256,1024]{1,0:T(8,128)(2,1)S(1)}, bf16[256,1024]{1,0:T(8,128)(2,1)}, u32[]{:S(2)}, u32[]{:S(2)}) collective-permute-start(bf16[256,1024]{1,0:T(8,128)(2,1)S(1)} %copy-done.8), channel_id=1, source_target_pairs={{0,8},{8,16},{16,24},{24,0},{1,9},{9,17},{17,25},{25,1},{2,10},{10... | collective-permute-start | bytes 1572872 | tf_op jit(solution)/shard_map/ppermute | solution.py:268
  557.5 121.8 %collective-permute-start.32 = (bf16[256,1024]{1,0:T(8,128)(2,1)S(1)}, bf16[256,1024]{1,0:T(8,128)(2,1)}, u32[]{:S(2)}, u32[]{:S(2)}) collective-permute-start(bf16[256,1024]{1,0:T(8,128)(2,1)S(1)} %copy-done.7), channel_id=1, source_target_pairs={{0,24},{8,0},{16,8},{24,16},{1,25},{9,1},{17,9},{25,17},{2,26},{10... | collective-permute-start | bytes 1572872 | tf_op jit(solution)/shard_map/ppermute | solution.py:268
  558.3 121.9 %collective-permute-start.34 = (bf16[256,1024]{1,0:T(8,128)(2,1)S(1)}, bf16[256,1024]{1,0:T(8,128)(2,1)}, u32[]{:S(2)}, u32[]{:S(2)}) collective-permute-start(bf16[256,1024]{1,0:T(8,128)(2,1)S(1)} %copy-done.7), channel_id=1, source_target_pairs={{0,8},{8,16},{16,24},{24,0},{1,9},{9,17},{17,25},{25,1},{2,10},{10... | collective-permute-start | bytes 1572872 | tf_op jit(solution)/shard_map/ppermute | solution.py:268
  559.5 122.4 %collective-permute-start.35 = (bf16[256,1024]{1,0:T(8,128)(2,1)}, bf16[256,1024]{1,0:T(8,128)(2,1)}, u32[]{:S(2)}, u32[]{:S(2)}) collective-permute-start(bf16[256,1024]{1,0:T(8,128)(2,1)} %collective-permute-done.25.refs_10_.refs_3_), channel_id=1, source_target_pairs={{0,8},{8,16},{16,24},{24,0},{1,9},{9,17},{17,25},{25,1},{2,10},{10... | collective-permute-start | bytes 1572872 | tf_op jit(solution)/shard_map/ppermute | solution.py:268
  605.6 76.6 %collective-permute-start.30 = (bf16[256,1024]{1,0:T(8,128)(2,1)}, bf16[256,1024]{1,0:T(8,128)(2,1)S(1)}, u32[]{:S(2)}, u32[]{:S(2)}) collective-permute-start(bf16[256,1024]{1,0:T(8,128)(2,1)} %fusion.3.refs_0_), channel_id=1, source_target_pairs={{0,8},{8,16},{16,24},{24,0},{1,9},{9,17},{17,25},{25,1},{2,10},{10... | collective-permute-start | bytes 1572872 | tf_op jit(solution)/shard_map/ppermute | solution.py:268
  680.2 36.3 %collective-permute-start.29 = (bf16[256,1024]{1,0:T(8,128)(2,1)}, bf16[256,1024]{1,0:T(8,128)(2,1)S(1)}, u32[]{:S(2)}, u32[]{:S(2)}) collective-permute-start(bf16[256,1024]{1,0:T(8,128)(2,1)} %fusion.3.refs_0_), channel_id=1, source_target_pairs={{0,24},{8,0},{16,8},{24,16},{1,25},{9,1},{17,9},{25,17},{2,26},{10... | collective-permute-start | bytes 1572872 | tf_op jit(solution)/shard_map/ppermute | solution.py:268
  681.9 38.4 %collective-permute-start.28 = (bf16[256,1024]{1,0:T(8,128)(2,1)S(1)}, bf16[256,1024]{1,0:T(8,128)(2,1)S(1)}, u32[]{:S(2)}, u32[]{:S(2)}) collective-permute-start(bf16[256,1024]{1,0:T(8,128)(2,1)S(1)} %fusion.4.refs_0_), channel_id=1, source_target_pairs={{0,8},{8,16},{16,24},{24,0},{1,9},{9,17},{17,25},{25,1},{2,10},{10... | collective-permute-start | bytes 1572872 | tf_op jit(solution)/shard_map/ppermute | solution.py:268
  (60 other events, 772.0 us)
Sparse Core Ops, SparseCore 0:
  26.9 48.1 all-gather.5
  76.7 47.2 all-gather.7
  250.3 47.9 all-gather.9
  335.5 76.8 reduce-scatter.4
  420.3 95.9 reduce-scatter.6
  519.0 84.3 reduce-scatter.10
  605.7 72.0 reduce-scatter.8
